TPU v7x, 128 devices: a whole 4x4x4 slice. The times are simulated.
128 devices in a mesh: gx: 4 (over x), gy: 32 (over y, z, core).
Axes of the slice: x: 4, y: 4, z: 4, core: 2. Of those that a mesh axis runs over, the one named last changes fastest.
Arguments:
- replay_deter: float32 [32768, 2048], P(('gx', 'gy')), may hold values from -1 to 1
- replay_stoch: int32 [32768, 32], P(('gx', 'gy')), may hold values from 0 to 31
- send_rows: int32 [16384, 2], P(('gx', 'gy')), may hold values from 0 to 255
- send_counts: int32 [128, 128], P(('gx', 'gy')), may hold values from 0 to 2, as said below
- actions: int32 [32768, 4], P(('gx', 'gy')), may hold values from 0 to 17
- samples: int32 [32768, 4, 32], P(('gx', 'gy')), may hold values from 0 to 31
- w_stoch: bfloat16 [1024, 6144], P('gy'), may hold values from -1 to 1
- w_deter: bfloat16 [4, 512, 1536], P(None, 'gy'), may hold values from -0.25 to 0.25
- act_table: bfloat16 [18, 6144], replicated, may hold values from -3 to 3
- w_prior: bfloat16 [2048, 1024], P('gy'), may hold values from -0.037353516 to 0.037353516
Outputs:
- imagined: bfloat16 [32768, 4, 2048], P(('gx', 'gy'))
- log_prob: float32 [32768, 4, 32], P(('gx', 'gy'))
Inputs may be any that keep to these rules, and one draw needn't show every extreme that they name: `send_rows`: entries past a destination's count are unused. `send_counts`: each source's counts sum to exactly 128; every source sends 2 rows to some owner, and some owner receives 2 rows from every source.
All inputs are finite; a program needn't handle non-finite values.
Results may differ from a plain program's by a relative error of at most 0.0022.
Values may be sent and summed in bfloat16 or wider, within the bound.
A program may use at most 128 MiB of HBM per device.

v0:
```python
import jax
import jax.numpy as jnp
from jax import lax
from jax.experimental import pallas as pl
from jax.experimental.pallas import tpu as pltpu
from jax.sharding import PartitionSpec as P

STEPS = 4
BLOCKS = 4
BF = jnp.bfloat16
F32 = jnp.float32
MESH = pl.DeviceIdType.MESH
SCALE = 32767.0


def dot(a, b, dims=((1,), (0,))):
    return lax.dot_general(a, b, (dims, ((), ())), preferred_element_type=F32)


def spread(rows, lanes):
    g = lax.broadcasted_iota(jnp.int32, (rows, lanes), 0)
    k = lax.broadcasted_iota(jnp.int32, (rows, lanes), 1)
    return jnp.where((k >= g * 32) & (k < g * 32 + 32), 1.0, 0.0).astype(BF)


def sig(v):
    return 0.5 * jnp.tanh(0.5 * v) + 0.5


def gru_kernel(
    deter, stoch_t, rows_t, counts, acts_t, samps_t, w_s, w_d, act, w_p,
    st_out, wp_out, live_out,
    WS, WD, WP, send, recv, send_z, recv_z, zf, H0, H, OH, ACT, PRE, ST,
    s_loc, s_snd, s_rcv, g_snd, g_rcv, f_snd, f_rcv, wp_snd, wp_rcv, d_snd, d_rcv, s_out,
):
    x = lax.axis_index("gx")
    gy = lax.axis_index("gy")
    y, z, c = gy // 8, (gy // 2) % 4, gy % 2
    me = x * 32 + gy

    def dev(tx, ty, tz, tc):
        return (tx, ty * 8 + tz * 2 + tc)

    def near(dim, step):
        s = (step + 4) % 4
        if dim == "x":
            return dev((x + s) % 4, y, z, c)
        if dim == "y":
            return dev(x, (y + s) % 4, z, c)
        return dev(x, y, (z + s) % 4, c)

    pos = {"x": x, "y": y, "z": z}
    partner = dev(x, y, z, 1 - c)

    def fill(b, wait):
        def go(src, dst, k):
            cp = pltpu.make_async_copy(src, dst, s_loc.at[k])
            if not wait:
                cp.start()

        for p in range(3):
            for q in range(4) if p == 0 else (x,):
                col = pl.multiple_of(b * 1536 + p * 512 + q * 128, 128)
                go(w_s.at[:, pl.ds(col, 128)], WS.at[b, p, q, y, z, c], 0)
                col2 = pl.multiple_of(p * 512 + q * 128, 128)
                go(w_d.at[b, :, pl.ds(col2, 128)], WD.at[b, p, q, y, z, c], 1)
        return 0

    lax.fori_loop(0, 4, lambda b, u: fill(b, False), 0)
    for j in range(8):
        if j < 3:
            for q in range(4):
                pltpu.make_async_copy(
                    w_p.at[pl.ds(q * 16, 16), pl.ds(j * 128, 128)], WP.at[j, y, z, c, q], s_loc.at[2]
                ).start()
        else:
            pltpu.make_async_copy(
                w_p.at[pl.ds(pl.multiple_of(x * 16, 16), 16), pl.ds(j * 128, 128)],
                WP.at[j, y, z, c, x],
                s_loc.at[3],
            ).start()

    iota = lax.broadcasted_iota(jnp.int32, (256, 128), 0)
    sel_t = jnp.concatenate(
        [jnp.where(iota == rows_t[i : i + 1, :], 1.0, 0.0) for i in range(2)], axis=1
    )
    sel = jnp.transpose(sel_t).astype(BF)
    for k in range(8):
        lo = 512 * (k // 2) + 128 * (k % 2)
        parts = []
        for col in (lo, lo + 256):
            code = jnp.round(deter[:, col : col + 128] * SCALE)
            high = jnp.floor(code * (1.0 / 256.0))
            parts += [high.astype(BF), (code - high * 256.0).astype(BF)]
        got = dot(sel, jnp.concatenate(parts, axis=1))
        v0 = (got[:, 0:128] * 256.0 + got[:, 128:256]).astype(jnp.int32)
        v1 = (got[:, 256:384] * 256.0 + got[:, 384:512]).astype(jnp.int32)
        word = v1 * 65536 + (v0 + 32768)
        send[pl.ds(k, 128, stride=16), :] = word[0:128]
        send[pl.ds(8 + k, 128, stride=16), :] = word[128:256]
    picked = dot(stoch_t[...].astype(F32).astype(BF), sel_t.astype(BF))
    zs = [
        jnp.where(counts[...] > i, picked[:, 128 * i : 128 * i + 128], 64.0) for i in range(2)
    ]
    zs = jnp.concatenate(zs + [jnp.zeros((64, 128), F32)], axis=0)
    send_z[...] = jnp.transpose(zs).astype(jnp.int32).reshape(128, 1, 128)

    def wait_bytes(ref, sem):
        pltpu.make_async_copy(ref, ref, sem).wait()

    wait_bytes(WS.at[0, :, :, 0:2, 0, 0], s_loc.at[0])
    wait_bytes(WD.at[0, :, :, 0:2, 0, 0], s_loc.at[1])
    wait_bytes(WP.at[0:3, 0, 0, 0], s_loc.at[2])
    wait_bytes(WP.at[0:5, 0, 0, 0, 0], s_loc.at[3])

    def copy_to(ref, snd, rcv, to):
        return pltpu.make_async_remote_copy(
            src_ref=ref, dst_ref=ref, send_sem=snd, recv_sem=rcv, device_id=to, device_id_type=MESH
        )

    class Ring:
        def __init__(self, dim, part, half, snd, rcv):
            self.dim, self.part, self.half, self.snd, self.rcv = dim, part, half, snd, rcv

        def at(self, step):
            return (pos[self.dim] + step + 4) % 4

        def copy(self, k):
            if k < 2:
                ref = self.part(self.at(0))
            else:
                ref = self.half(self.at(-1 if k == 2 else 1), k - 2)
            return copy_to(ref, self.snd.at[k], self.rcv.at[k], near(self.dim, 1 if k % 2 == 0 else -1))

        def came(self, k):
            if k < 2:
                ref = self.part(self.at(-1 if k == 0 else 1))
            else:
                ref = self.half(self.at(2), k - 2)
            return copy_to(ref, self.snd.at[k], self.rcv.at[k], near(self.dim, 1 if k % 2 == 0 else -1))

        def start(self):
            self.copy(0).start()
            self.copy(1).start()

        def mid(self):
            for k in range(2):
                self.came(k).wait_recv()
                self.copy(2 + k).start()

        def end(self):
            for k in range(2):
                self.came(2 + k).wait_recv()

        def sent(self):
            for k in range(4):
                self.copy(k).wait_send()

    def early(i, dim, parts):
        return [Ring(dim, part, half, g_snd.at[i, a], g_rcv.at[i, a]) for a, (part, half) in enumerate(parts)]

    hs = (slice(0, 2), slice(2, 4))
    a_y = early(0, "y", [
        (lambda i: WS.at[:, 0, :, i, z, c], lambda i, h: WS.at[hs[h], 0, :, i, z, c]),
        (lambda i: WD.at[:, 0, :, i, z, c], lambda i, h: WD.at[hs[h], 0, :, i, z, c]),
        (lambda i: WP.at[0:3, i, z, c], lambda i, h: WP.at[0:3, i, z, c, hs[h]]),
    ])
    b_y = early(1, "y", [
        (lambda i: WS.at[:, 1, x, i, z, c], lambda i, h: WS.at[hs[h], 1, x, i, z, c]),
        (lambda i: WD.at[:, 1, x, i, z, c], lambda i, h: WD.at[hs[h], 1, x, i, z, c]),
        (lambda i: WP.at[3:6, i, z, c, x], lambda i, h: WP.at[slice(3, 4) if h == 0 else slice(4, 6), i, z, c, x]),
    ])
    c_z = early(2, "z", [
        (lambda i: WS.at[:, 2, x, y, i, c], lambda i, h: WS.at[hs[h], 2, x, y, i, c]),
        (lambda i: WD.at[:, 2, x, y, i, c], lambda i, h: WD.at[hs[h], 2, x, y, i, c]),
        (lambda i: WP.at[6:8, y, i, c, x], lambda i, h: WP.at[6 + h : 7 + h, y, i, c, x]),
    ])
    b_z = early(3, "z", [
        (lambda i: WS.at[:, 1, x, :, i, c], lambda i, h: WS.at[hs[h], 1, x, :, i, c]),
        (lambda i: WD.at[:, 1, x, :, i, c], lambda i, h: WD.at[hs[h], 1, x, :, i, c]),
        (lambda i: WP.at[3:6, :, i, c, x], lambda i, h: WP.at[3:6, hs[h], i, c, x]),
    ])
    c_x = early(4, "x", [
        (lambda i: WS.at[:, 2, i, y, :, c], lambda i, h: WS.at[hs[h], 2, i, y, :, c]),
        (lambda i: WD.at[:, 2, i, y, :, c], lambda i, h: WD.at[hs[h], 2, i, y, :, c]),
        (lambda i: WP.at[6:8, y, :, c, i], lambda i, h: WP.at[6:8, y, hs[h], c, i]),
    ])

    def last(W, b, s):
        sn, rc = f_snd.at[b], f_rcv.at[b]
        return [
            Ring("z", lambda i: W.at[b, 0, :, :, i, c], lambda i, h: W.at[b, 0, hs[h], :, i, c], sn.at[0, s], rc.at[0, s]),
            Ring("x", lambda i: W.at[b, 1, i, :, :, c], lambda i, h: W.at[b, 1, i, hs[h], :, c], sn.at[1, s], rc.at[1, s]),
            Ring("y", lambda i: W.at[b, 2, :, i, :, c], lambda i, h: W.at[b, 2, hs[h], i, :, c], sn.at[2, s], rc.at[2, s]),
        ]

    def last_p():
        return [
            Ring("z", lambda i: WP.at[0:3, :, i, c], lambda i, h: WP.at[0:3, hs[h], i, c], wp_snd.at[0], wp_rcv.at[0]),
            Ring("x", lambda i: WP.at[3:6, :, :, c, i], lambda i, h: WP.at[3:6, hs[h], :, c, i], wp_snd.at[1], wp_rcv.at[1]),
            Ring("y", lambda i: WP.at[6:8, i, :, c], lambda i, h: WP.at[6:8, i, hs[h], c], wp_snd.at[2], wp_rcv.at[2]),
        ]

    class Block:
        def __init__(self, rings, whole):
            self.rings = rings
            self.whole = whole

        def over(self, ref, k):
            copy_to(ref, d_snd.at[k], d_rcv.at[k], partner).start()

        def start(self):
            for r, k in self.rings:
                r.start()
                self.over(r.part(r.at(0)), k)

        def mid(self):
            for r, k in self.rings:
                for e in range(2):
                    r.came(e).wait_recv()
                    r.copy(2 + e).start()
                    self.over(r.part(r.at(-1 if e == 0 else 1)), k)

        def end(self):
            for r, k in self.rings:
                for e in range(2):
                    r.came(2 + e).wait_recv()
                    self.over(r.half(r.at(2), e), k)

        def ready(self):
            for ref, k in self.whole:
                wait_bytes(ref(1 - c), d_rcv.at[k])

        def sent(self):
            for r, _ in self.rings:
                r.sent()
            for ref, k in self.whole:
                wait_bytes(ref(c), d_snd.at[k])

    def block(b):
        return Block(
            [(r, 2 * b) for r in last(WS, b, 0)] + [(r, 2 * b + 1) for r in last(WD, b, 1)],
            [(lambda e: WS.at[b, :, :, :, :, e], 2 * b), (lambda e: WD.at[b, :, :, :, :, e], 2 * b + 1)],
        )

    def block_p():
        return Block([(r, 8) for r in last_p()], [(lambda e: WP.at[:, :, :, e], 8)])

    for r in b_y + c_z + a_y:
        r.start()

    def rows_of(n):
        return pl.ds(pl.multiple_of(n * 16, 16), 16)

    def a2a(i):
        r = i % 32
        tx, ty, tz, tc = (x + i // 32) % 4, (y + r // 8) % 4, (z + (r // 2) % 4) % 4, (c + r % 2) % 2
        to = dev(tx, ty, tz, tc)
        n = tx * 32 + ty * 8 + tz * 2 + tc
        return (
            pltpu.make_async_remote_copy(
                src_ref=send.at[rows_of(n), :], dst_ref=recv.at[rows_of(me), :],
                send_sem=s_snd.at[0], recv_sem=s_rcv.at[0], device_id=to, device_id_type=MESH,
            ),
            pltpu.make_async_remote_copy(
                src_ref=send_z.at[n], dst_ref=recv_z.at[me],
                send_sem=s_snd.at[1], recv_sem=s_rcv.at[1], device_id=to, device_id_type=MESH,
            ),
        )

    def a2a_start(i, u):
        for cp in a2a(i):
            cp.start()
        return u

    lax.fori_loop(1, 128, a2a_start, 0)
    own = [
        pltpu.make_async_copy(send.at[rows_of(me), :], recv.at[rows_of(me), :], s_loc.at[4]),
        pltpu.make_async_copy(send_z.at[me], recv_z.at[me], s_loc.at[5]),
    ]
    for cp in own:
        cp.start()

    for r in b_y + c_z:
        r.mid()
    for r in b_y + c_z:
        r.end()
    for r in b_z + c_x:
        r.start()
    for r in a_y:
        r.mid()
    for r in a_y:
        r.end()

    E = spread(32, 1024)
    cls = (lax.broadcasted_iota(jnp.int32, (256, 1024), 1) % 32).astype(F32)
    for t in range(1, 4):
        rep = dot(samps_t[t - 1].astype(F32).astype(BF), E, ((0,), (0,)))
        OH[t] = jnp.where(rep == cls, 1.0, 0.0).astype(BF)
    ACT[...] = jnp.zeros_like(ACT)
    ACT[0 : act.shape[0], :] = act[...]

    for r in b_z + c_x:
        r.mid()
    for r in b_z + c_x:
        r.end()
    block(0).start()
    block(1).start()

    wait_bytes(recv.at[pl.ds(0, 127 * 16), :], s_rcv.at[0])
    wait_bytes(recv_z.at[pl.ds(0, 127)], s_rcv.at[1])
    for cp in own:
        cp.wait()
    zv = recv_z[...].reshape(128, 128)
    zf[pl.ds(0, 128, stride=2), :] = zv
    zf[pl.ds(1, 128, stride=2), :] = pltpu.roll(zv, 96, 1)
    codes = zf[...].astype(F32)
    rep = dot(codes[:, 0:32].astype(BF), E)
    OH[0] = jnp.where(rep == cls, 1.0, 0.0).astype(BF)
    alive = jnp.where(codes < 32.0, 1.0, 0.0)
    lane0 = jnp.where(lax.broadcasted_iota(jnp.int32, (8, 128), 1) == 0, 1.0, 0.0).astype(BF)
    live_out[...] = dot(lane0, alive.astype(BF), ((1,), (1,)))
    live_col = alive[:, 0:1]
    for k in range(8):
        word = recv[pl.ds(k, 256, stride=8), :]
        v1 = lax.shift_right_arithmetic(word, 16)
        v0 = (word & 65535) - 32768
        b, e = k // 2, (k % 2) * 128
        H0[b, :, e : e + 128] = v0.astype(F32) * (1.0 / SCALE)
        H0[b, :, 256 + e : 384 + e] = v1.astype(F32) * (1.0 / SCALE)

    block(0).mid()
    block(0).end()
    block(0).ready()

    def compute(b, u):
        def gate(p):
            def pre(t, u):
                rhs = jnp.concatenate([WS[b, p, q].reshape(1024, 128) for q in range(4)], axis=1)
                a_hot = jnp.where(
                    lax.broadcasted_iota(jnp.int32, (32, 256), 0) == acts_t[pl.ds(t, 1), :], 1.0, 0.0
                ).astype(BF)
                cols = pl.ds(pl.multiple_of(b * 1536 + p * 512, 512), 512)
                PRE[t, p] = dot(OH[t], rhs) + dot(a_hot, ACT[:, cols], ((0,), (0,)))
                return u

            lax.fori_loop(0, STEPS, pre, 0)

        gate(0)

        @pl.when(b < 2)
        def _():
            block(b + 2).start()

        @pl.when(b == 2)
        def _():
            block_p().start()

        gate(1)

        @pl.when(b < 3)
        def _():
            block(b + 1).mid()

        @pl.when(b == 3)
        def _():
            block_p().mid()

        gate(2)
        H[...] = H0[b]

        def step(t, u):
            h = H[...]
            low = h.astype(BF)

            def gates(p):
                rhs = jnp.concatenate([WD[b, p, q].reshape(512, 128) for q in range(4)], axis=1)
                return PRE[t, p] + dot(low, rhs)

            cand = jnp.tanh(sig(gates(0)) * gates(1))
            g = sig(gates(2) - 1.0)
            new = g * cand + (1.0 - g) * h
            H[...] = new
            ST[b, t] = (new * live_col).astype(BF)
            return u

        lax.fori_loop(0, STEPS, step, 0)
        pltpu.make_async_copy(ST.at[b], st_out.at[b], s_out.at[b]).start()

        @pl.when(b < 3)
        def _():
            block(b + 1).end()
            block(b + 1).ready()

        return u

    lax.fori_loop(0, BLOCKS, compute, 0)
    bp = block_p()
    bp.end()
    bp.ready()
    out_p = pltpu.make_async_copy(WP, wp_out, s_out.at[4])
    out_p.start()
    for r in a_y + b_y + c_z + b_z + c_x:
        r.sent()
    wait_bytes(send.at[pl.ds(0, 127 * 16), :], s_snd.at[0])
    wait_bytes(send_z.at[pl.ds(0, 127)], s_snd.at[1])

    def drain(b, u):
        block(b).sent()
        pltpu.make_async_copy(ST.at[b], st_out.at[b], s_out.at[b]).wait()
        return u

    lax.fori_loop(0, BLOCKS, drain, 0)
    bp.sent()
    out_p.wait()


def prior_kernel(st, wp, live, samps_t, out):
    E = spread(32, 1024)
    cls = (lax.broadcasted_iota(jnp.int32, (256, 1024), 1) % 32).astype(F32)

    def step(t, u):
        logits = jnp.zeros((256, 1024), F32)
        for b in range(BLOCKS):
            rhs = jnp.concatenate([wp[j, b].reshape(512, 128) for j in range(8)], axis=1)
            logits = logits + dot(st[b, t], rhs)
        rep = dot(samps_t[t].astype(F32).astype(BF), E, ((0,), (0,)))

        def grouped(v):
            hi = v.astype(BF)
            lo = (v - hi.astype(F32)).astype(BF)
            return dot(E, hi, ((1,), (1,))) + dot(E, lo, ((1,), (1,)))

        total = jnp.log(grouped(jnp.exp(logits)))
        hit = grouped(jnp.where(rep == cls, logits, 0.0))
        out[t] = jnp.where(live[0:1, :] > 0.0, hit - total, 0.0)
        return u

    lax.fori_loop(0, STEPS, step, 0)


def on_device(deter, stoch, rows, counts, acts, samps, w_s, w_d, act, w_p):
    vmem = pl.BlockSpec(memory_space=pltpu.VMEM)
    hbm = pl.BlockSpec(memory_space=pl.ANY)
    dma = pltpu.SemaphoreType.DMA
    samps_t = samps.transpose(1, 2, 0)
    states, wp, live = pl.pallas_call(
        gru_kernel,
        name="gru",
        out_shape=(
            jax.ShapeDtypeStruct((4, 4, 256, 512), BF),
            jax.ShapeDtypeStruct((8, 4, 4, 2, 4, 16, 128), BF),
            jax.ShapeDtypeStruct((8, 256), F32),
        ),
        in_specs=[vmem] * 6 + [hbm, hbm, vmem, hbm],
        out_specs=(hbm, hbm, vmem),
        scratch_shapes=[
            pltpu.VMEM((4, 3, 4, 4, 4, 2, 32, 128), BF),
            pltpu.VMEM((4, 3, 4, 4, 4, 2, 16, 128), BF),
            pltpu.VMEM((8, 4, 4, 2, 4, 16, 128), BF),
            pltpu.VMEM((2048, 128), jnp.int32),
            pltpu.VMEM((2048, 128), jnp.int32),
            pltpu.VMEM((128, 1, 128), jnp.int32),
            pltpu.VMEM((128, 1, 128), jnp.int32),
            pltpu.VMEM((256, 128), jnp.int32),
            pltpu.VMEM((4, 256, 512), F32),
            pltpu.VMEM((256, 512), F32),
            pltpu.VMEM((4, 256, 1024), BF),
            pltpu.VMEM((32, 6144), BF),
            pltpu.VMEM((4, 3, 256, 512), F32),
            pltpu.VMEM((4, 4, 256, 512), BF),
            dma((6,)), dma((2,)), dma((2,)),
            dma((5, 3, 4)), dma((5, 3, 4)),
            dma((4, 3, 2, 4)), dma((4, 3, 2, 4)),
            dma((3, 4)), dma((3, 4)),
            dma((9,)), dma((9,)), dma((5,)),
        ],
        compiler_params=pltpu.CompilerParams(
            has_side_effects=True, vmem_limit_bytes=60 * 1024 * 1024
        ),
    )(deter, stoch.T, rows.T, counts, acts.T, samps_t, w_s, w_d, act, w_p)
    imagined = states.transpose(2, 1, 0, 3).reshape(256, 4, 2048)
    logp = pl.pallas_call(
        prior_kernel,
        name="prior",
        out_shape=jax.ShapeDtypeStruct((4, 32, 256), F32),
        in_specs=[vmem] * 4,
        out_specs=vmem,
        compiler_params=pltpu.CompilerParams(vmem_limit_bytes=48 * 1024 * 1024),
    )(states, wp, live, samps_t)
    return (imagined, logp.transpose(2, 0, 1))


def solution(mesh):
    in_specs = (
        P(("gx", "gy"), None),
        P(("gx", "gy"), None),
        P(("gx", "gy"), None),
        P(("gx", "gy"), None),
        P(("gx", "gy"), None),
        P(("gx", "gy"), None, None),
        P("gy", None),
        P(None, "gy", None),
        P(),
        P("gy", None),
    )
    out_specs = (P(("gx", "gy"), None, None), P(("gx", "gy"), None, None))
    return jax.shard_map(
        on_device, mesh=mesh, in_specs=in_specs, out_specs=out_specs, check_vma=False
    )
```

profile of v0, /device:TPU:1, one launch (start us, length us, event | category | flops | bytes accessed | tf_op | source)
XLA Modules:
  0.0 146.0 jit_solution(16306278972087559354)
XLA Ops:
  0.6 115.4 %gru.1 = (bf16[4,4,256,512]{3,2,1,0:T(8,128)(2,1)}, bf16[8,4,4,2,4,16,128]{6,5,4,3,2,1,0:T(8,128)(2,1)}, f32[8,256]{1,0:T(8,128)}) custom-call(f32[256,2048]{1,0:T(8,128)} %deter.1, s32[32,256]{1,0:T(8,128)} %bitcast.12, s32[2,128]{1,0:T(2,128)} %bitcast.14, s32[1,128]{1,0:T(1,128)} %counts.1, s32[4,256]{1,0:T(4,128)} %bitcast.13, s32[4,32,256]{2,1,0:T(8,128)} %bitcast.8, ...), custom_call_target="tpu_custom_call" | custom-call | tf_op jit(solution)/shard_map/gru/pallas_call | solution.py:447
  116.1 0.0 copy-start
  116.1 2.2 %copy-done = bf16[4,4,256,512]{3,2,1,0:T(8,128)(2,1)S(1)} copy-done((bf16[4,4,256,512]{3,2,1,0:T(8,128)(2,1)S(1)}, bf16[4,4,256,512]{3,2,1,0:T(8,128)(2,1)}, u32[]{:S(2)}) %copy-start) | copy-done | bytes 4194328
  118.3 0.0 copy-start.1
  118.3 0.9 copy-done.1
  119.2 0.0 copy-start.2
  119.2 0.7 copy-done.2
  119.9 11.0 %prior.1 = f32[4,32,256]{2,1,0:T(8,128)} custom-call(bf16[4,4,256,512]{3,2,1,0:T(8,128)(2,1)S(1)} %copy-done, bf16[8,4,4,2,4,16,128]{6,5,4,3,2,1,0:T(8,128)(2,1)} %get-tuple-element.6.wp, f32[8,256]{1,0:T(8,128)S(1)} %copy-done.2, s32[4,32,256]{2,1,0:T(8,128)S(1)} %bitcast.9), custom_call_target="tpu_custom_call" | custom-call | tf_op jit(solution)/shard_map/prior/pallas_call | solution.py:483
  130.9 7.3 %copy.12 = bf16[256,4,4,512]{0,3,2,1:T(8,128)(2,1)} copy(bf16[256,4,4,512]{3,0,1,2:T(8,128)(2,1)} %bitcast.7) | data formatting | bytes 8388608 | tf_op jit(solution)/shard_map/transpose | solution.py:482
  138.2 7.8 %copy.13 = bf16[256,4,2048]{2,1,0:T(4,128)(2,1)} copy(bf16[256,4,2048]{0,2,1:T(8,128)(2,1)} %bitcast.10) | data formatting | bytes 8388608
Async XLA Ops:
  116.1 2.2 %copy-start = (bf16[4,4,256,512]{3,2,1,0:T(8,128)(2,1)S(1)}, bf16[4,4,256,512]{3,2,1,0:T(8,128)(2,1)}, u32[]{:S(2)}) copy-start(bf16[4,4,256,512]{3,2,1,0:T(8,128)(2,1)} %get-tuple-element.5.st) | copy-start | bytes 12582916
  118.3 0.9 copy-start.1
  119.2 0.7 copy-start.2
where the time goes:
time: 147 us; the launch traced here: 146 us
  Pallas kernels  126 us (86%)
  local copies, waits for them, and re-layouts  18.9 us (13%)
    pallas_call x1, Pallas kernels, on_device(): pl.pallas_call(gru_kernel, name='gru', out_shape=(jax.ShapeDtypeStruct((4...  115 us
    unnamed x7, local copies, waits for them, and re-layouts  11.6 us
    pallas_call x1, Pallas kernels, on_device(): pl.pallas_call(prior_kernel, name='prior', out_shape=jax.ShapeDtypeStruct...  11 us
    transpose x1, local copies, waits for them, and re-layouts, on_device(): imagined = states.transpose(2, 1, 0, 3).reshape(256, 4, 2048)  7.3 us

commit v1 on v0

v1 whole, which is shorter than its diff:
```python
import jax
import jax.numpy as jnp
from jax import lax
from jax.experimental import pallas as pl
from jax.experimental.pallas import tpu as pltpu
from jax.sharding import PartitionSpec as P

STEPS = 4
BLOCKS = 4
BF = jnp.bfloat16
F32 = jnp.float32
MESH = pl.DeviceIdType.MESH
SCALE = 32767.0


def dot(a, b, dims=((1,), (0,))):
    return lax.dot_general(a, b, (dims, ((), ())), preferred_element_type=F32)


def spread(rows, lanes):
    g = lax.broadcasted_iota(jnp.int32, (rows, lanes), 0)
    k = lax.broadcasted_iota(jnp.int32, (rows, lanes), 1)
    return jnp.where((k >= g * 32) & (k < g * 32 + 32), 1.0, 0.0).astype(BF)


def sig(v):
    return 0.5 * jnp.tanh(0.5 * v) + 0.5


def gru_kernel(
    deter_h, stoch_t, rows_t, counts, acts_t, samps_t, w_s, w_d, act, w_p,
    st_out, wp_out, live_out,
    deter, WS, WD, WP, send, recv, send_z, recv_z, zf, H0, H, OH, ACT, PRE, ST,
    s_loc, s_snd, s_rcv, w_snd, w_rcv, p_snd, p_rcv, d_snd, d_rcv, s_out,
):
    x = lax.axis_index("gx")
    gy = lax.axis_index("gy")
    y, z, c = gy // 8, (gy // 2) % 4, gy % 2
    me = x * 32 + gy

    def dev(tx, ty, tz, tc):
        return (tx, ty * 8 + tz * 2 + tc)

    def near(dim, step):
        s = (step + 4) % 4
        if dim == "x":
            return dev((x + s) % 4, y, z, c)
        if dim == "y":
            return dev(x, (y + s) % 4, z, c)
        return dev(x, y, (z + s) % 4, c)

    pos = {"x": x, "y": y, "z": z}
    partner = dev(x, y, z, 1 - c)

    def wait_bytes(ref, sem):
        pltpu.make_async_copy(ref, ref, sem).wait()

    get_deter = pltpu.make_async_copy(deter_h, deter, s_loc.at[6])

    def fill(b, u):
        for p in range(3):
            for q in range(4) if p == 0 else (x,):
                col = pl.multiple_of(b * 1536 + p * 512 + q * 128, 128)
                pltpu.make_async_copy(
                    w_s.at[:, pl.ds(col, 128)], WS.at[b, p, q, y, z, c], s_loc.at[0]
                ).start()
                col = pl.multiple_of(p * 512 + q * 128, 128)
                pltpu.make_async_copy(
                    w_d.at[b, :, pl.ds(col, 128)], WD.at[b, p, q, y, z, c], s_loc.at[1]
                ).start()
        return u

    lax.fori_loop(0, 4, fill, 0)
    for j in range(8):
        if j < 3:
            for q in range(4):
                pltpu.make_async_copy(
                    w_p.at[pl.ds(q * 16, 16), pl.ds(j * 128, 128)], WP.at[j, y, z, c, q], s_loc.at[2]
                ).start()
        else:
            pltpu.make_async_copy(
                w_p.at[pl.ds(pl.multiple_of(x * 16, 16), 16), pl.ds(j * 128, 128)],
                WP.at[j, y, z, c, x],
                s_loc.at[3],
            ).start()
    get_deter.start()

    iota = lax.broadcasted_iota(jnp.int32, (256, 128), 0)
    sel_t = jnp.concatenate(
        [jnp.where(iota == rows_t[i : i + 1, :], 1.0, 0.0) for i in range(2)], axis=1
    )
    sel = jnp.transpose(sel_t).astype(BF)
    picked = dot(stoch_t[...].astype(F32).astype(BF), sel_t.astype(BF))
    zs = [
        jnp.where(counts[...] > i, picked[:, 128 * i : 128 * i + 128], 64.0) for i in range(2)
    ]
    zs = jnp.concatenate(zs + [jnp.zeros((64, 128), F32)], axis=0)
    send_z[...] = jnp.transpose(zs).astype(jnp.int32).reshape(128, 1, 128)

    wait_bytes(WS.at[0, :, :, 0:2, 0, 0], s_loc.at[0])
    wait_bytes(WD.at[0, :, :, 0:2, 0, 0], s_loc.at[1])
    wait_bytes(WP.at[0:3, 0, 0, 0], s_loc.at[2])
    wait_bytes(WP.at[0:5, 0, 0, 0, 0], s_loc.at[3])

    def copy_to(ref, snd, rcv, to):
        return pltpu.make_async_remote_copy(
            src_ref=ref, dst_ref=ref, send_sem=snd, recv_sem=rcv, device_id=to, device_id_type=MESH
        )

    class Ring:
        def __init__(self, dim, part, half, snd, rcv, solo=False):
            self.dim, self.part, self.half, self.snd, self.rcv = dim, part, half, snd, rcv
            self.far = (2,) if solo else (2, 3)

        def at(self, step):
            return (pos[self.dim] + step + 4) % 4

        def make(self, ref, k):
            return copy_to(ref, self.snd(k), self.rcv.at[k], near(self.dim, 1 if k % 2 == 0 else -1))

        def start(self):
            for k in range(2):
                self.make(self.part(self.at(0)), k).start()

        def mid(self, then=None):
            for k in range(2):
                side = self.part(self.at(-1 if k == 0 else 1))
                self.make(side, k).wait_recv()
                if k + 2 in self.far:
                    self.make(self.half(self.at(-1 if k == 0 else 1), k), k + 2).start()
                if then is not None:
                    then(side)

        def end(self, then=None):
            for k in self.far:
                far = self.half(self.at(2), k - 2)
                self.make(far, k).wait_recv()
                if then is not None:
                    then(far)

    hs = (slice(0, 2), slice(2, 4))

    def rings(W, b, s):
        rows = 32 if s == 0 else 16

        def ring(n, dim, part, half, group, solo=False):
            return Ring(dim, part, half, lambda k: w_snd.at[b, s, group], w_rcv.at[b, s, n], solo)

        def split(ref, h):
            return ref if s == 1 else ref.at[pl.ds(16 * h, 16)]

        return {
            "ay": ring(0, "y", lambda i: W.at[b, 0, :, i, z, c], lambda i, h: W.at[b, 0, hs[h], i, z, c], 1),
            "by": ring(1, "y", lambda i: W.at[b, 1, x, i, z, c], lambda i, h: split(W.at[b, 1, x, i, z, c], h), 0, s == 1),
            "cz": ring(2, "z", lambda i: W.at[b, 2, x, y, i, c], lambda i, h: split(W.at[b, 2, x, y, i, c], h), 0, s == 1),
            "bz": ring(3, "z", lambda i: W.at[b, 1, x, :, i, c], lambda i, h: W.at[b, 1, x, hs[h], i, c], 1),
            "cx": ring(4, "x", lambda i: W.at[b, 2, i, y, :, c], lambda i, h: W.at[b, 2, i, y, hs[h], c], 1),
            "fz": ring(5, "z", lambda i: W.at[b, 0, :, :, i, c], lambda i, h: W.at[b, 0, hs[h], :, i, c], 2),
            "fx": ring(6, "x", lambda i: W.at[b, 1, i, :, :, c], lambda i, h: W.at[b, 1, i, hs[h], :, c], 2),
            "fy": ring(7, "y", lambda i: W.at[b, 2, :, i, :, c], lambda i, h: W.at[b, 2, hs[h], i, :, c], 2),
        }

    def rings_p():
        def ring(n, dim, part, half):
            return Ring(dim, part, half, lambda k: p_snd.at[n, k], p_rcv.at[n])

        return {
            "ay": ring(0, "y", lambda i: WP.at[0:3, i, z, c], lambda i, h: WP.at[0:3, i, z, c, hs[h]]),
            "by": ring(1, "y", lambda i: WP.at[3:6, i, z, c, x], lambda i, h: WP.at[3 + h : 4 + 2 * h, i, z, c, x]),
            "cz": ring(2, "z", lambda i: WP.at[6:8, y, i, c, x], lambda i, h: WP.at[6 + h : 7 + h, y, i, c, x]),
            "bz": ring(3, "z", lambda i: WP.at[3:6, :, i, c, x], lambda i, h: WP.at[3:6, hs[h], i, c, x]),
            "cx": ring(4, "x", lambda i: WP.at[6:8, y, :, c, i], lambda i, h: WP.at[6:8, y, hs[h], c, i]),
            "fz": ring(5, "z", lambda i: WP.at[0:3, :, i, c], lambda i, h: WP.at[0:3, hs[h], i, c]),
            "fx": ring(6, "x", lambda i: WP.at[3:6, :, :, c, i], lambda i, h: WP.at[3:6, hs[h], :, c, i]),
            "fy": ring(7, "y", lambda i: WP.at[6:8, i, :, c], lambda i, h: WP.at[6:8, i, hs[h], c]),
        }

    def over(k):
        def go(ref):
            copy_to(ref, d_snd.at[k], d_rcv.at[k], partner).start()

        return go

    def stage(n, b):
        if isinstance(b, int) and b == 4:
            sets = [(rings_p(), over(8))]
        else:
            sets = [(rings(WS, b, 0), over(2 * b)), (rings(WD, b, 1), over(2 * b + 1))]

        def each(names, what, hand=False):
            for name in names:
                for r, give in sets:
                    what(r[name], give if hand else None)

        def start(r, give):
            r.start()
            if give is not None:
                give(r.part(r.at(0)))

        if n == 1:
            each(("by", "cz", "ay"), start)
        elif n == 2:
            each(("by", "cz", "ay"), Ring.mid)
        elif n == 3:
            each(("by", "cz"), Ring.end)
            each(("bz", "cx"), start)
        elif n == 4:
            each(("bz", "cx"), Ring.mid)
            each(("ay",), Ring.end)
            each(("fz",), start, True)
        elif n == 5:
            each(("bz", "cx"), Ring.end)
            each(("fx", "fy"), start, True)
        elif n == 6:
            each(("fz", "fx", "fy"), Ring.mid, True)
        else:
            each(("fz", "fx", "fy"), Ring.end, True)

    def ready(b):
        wait_bytes(WS.at[b, :, :, :, :, 1 - c], d_rcv.at[2 * b])
        wait_bytes(WD.at[b, :, :, :, :, 1 - c], d_rcv.at[2 * b + 1])

    stage(1, 0)
    stage(1, 1)

    get_deter.wait()
    for k in range(8):
        lo = 512 * (k // 2) + 128 * (k % 2)
        parts = []
        for col in (lo, lo + 256):
            code = jnp.round(deter[:, col : col + 128] * SCALE)
            high = jnp.floor(code * (1.0 / 256.0))
            parts += [high.astype(BF), (code - high * 256.0).astype(BF)]
        got = dot(sel, jnp.concatenate(parts, axis=1))
        v0 = (got[:, 0:128] * 256.0 + got[:, 128:256]).astype(jnp.int32)
        v1 = (got[:, 256:384] * 256.0 + got[:, 384:512]).astype(jnp.int32)
        word = v1 * 65536 + (v0 + 32768)
        send[pl.ds(k, 128, stride=16), :] = word[0:128]
        send[pl.ds(8 + k, 128, stride=16), :] = word[128:256]
        if k == 4:
            stage(2, 0)
            stage(1, 2)

    stage(3, 0)
    stage(2, 1)

    def rows_of(n):
        return pl.ds(pl.multiple_of(n * 16, 16), 16)

    def a2a_start(i, u):
        r = i % 32
        tx, ty, tz, tc = (x + i // 32) % 4, (y + r // 8) % 4, (z + (r // 2) % 4) % 4, (c + r % 2) % 2
        to = dev(tx, ty, tz, tc)
        n = tx * 32 + ty * 8 + tz * 2 + tc
        pltpu.make_async_remote_copy(
            src_ref=send.at[rows_of(n), :], dst_ref=recv.at[rows_of(me), :],
            send_sem=s_snd.at[0], recv_sem=s_rcv.at[0], device_id=to, device_id_type=MESH,
        ).start()
        pltpu.make_async_remote_copy(
            src_ref=send_z.at[n], dst_ref=recv_z.at[me],
            send_sem=s_snd.at[1], recv_sem=s_rcv.at[1], device_id=to, device_id_type=MESH,
        ).start()
        return u

    lax.fori_loop(1, 128, a2a_start, 0)
    own = [
        pltpu.make_async_copy(send.at[rows_of(me), :], recv.at[rows_of(me), :], s_loc.at[4]),
        pltpu.make_async_copy(send_z.at[me], recv_z.at[me], s_loc.at[5]),
    ]
    for cp in own:
        cp.start()

    E = spread(32, 1024)
    cls = (lax.broadcasted_iota(jnp.int32, (256, 1024), 1) % 32).astype(F32)

    def one_hot(t):
        rep = dot(samps_t[t - 1].astype(F32).astype(BF), E, ((0,), (0,)))
        OH[t] = jnp.where(rep == cls, 1.0, 0.0).astype(BF)

    stage(4, 0)
    stage(3, 1)
    stage(2, 2)
    stage(1, 3)
    one_hot(1)
    ACT[...] = jnp.zeros_like(ACT)
    ACT[0 : act.shape[0], :] = act[...]
    stage(5, 0)
    stage(4, 1)
    stage(3, 2)
    stage(2, 3)
    stage(1, 4)
    one_hot(2)
    one_hot(3)
    stage(6, 0)
    stage(5, 1)
    stage(4, 2)
    stage(3, 3)
    stage(2, 4)

    wait_bytes(recv_z.at[pl.ds(0, 127)], s_rcv.at[1])
    wait_bytes(recv.at[pl.ds(0, 127 * 16), :], s_rcv.at[0])
    for cp in own:
        cp.wait()
    zv = recv_z[...].reshape(128, 128)
    zf[pl.ds(0, 128, stride=2), :] = zv
    zf[pl.ds(1, 128, stride=2), :] = pltpu.roll(zv, 96, 1)
    codes = zf[...].astype(F32)
    rep = dot(codes[:, 0:32].astype(BF), E)
    OH[0] = jnp.where(rep == cls, 1.0, 0.0).astype(BF)
    alive = jnp.where(codes < 32.0, 1.0, 0.0)
    lane0 = jnp.where(lax.broadcasted_iota(jnp.int32, (8, 128), 1) == 0, 1.0, 0.0).astype(BF)
    live_out[...] = dot(lane0, alive.astype(BF), ((1,), (1,)))
    live_col = alive[:, 0:1]
    for k in range(8):
        word = recv[pl.ds(k, 256, stride=8), :]
        v1 = lax.shift_right_arithmetic(word, 16)
        v0 = (word & 65535) - 32768
        b, e = k // 2, (k % 2) * 128
        H0[b, :, e : e + 128] = v0.astype(F32) * (1.0 / SCALE)
        H0[b, :, 256 + e : 384 + e] = v1.astype(F32) * (1.0 / SCALE)

    stage(7, 0)
    stage(6, 1)
    stage(5, 2)
    stage(4, 3)
    stage(3, 4)
    ready(0)

    def compute(b, u):
        def gate(p):
            def pre(t, u):
                rhs = jnp.concatenate([WS[b, p, q].reshape(1024, 128) for q in range(4)], axis=1)
                a_hot = jnp.where(
                    lax.broadcasted_iota(jnp.int32, (32, 256), 0) == acts_t[pl.ds(t, 1), :], 1.0, 0.0
                ).astype(BF)
                cols = pl.ds(pl.multiple_of(b * 1536 + p * 512, 512), 512)
                PRE[t, p] = dot(OH[t], rhs) + dot(a_hot, ACT[:, cols], ((0,), (0,)))
                return u

            lax.fori_loop(0, STEPS, pre, 0)

        gate(0)

        @pl.when(b < 2)
        def _():
            stage(6, b + 2)

        @pl.when(b == 2)
        def _():
            stage(6, 4)

        @pl.when(b == 0)
        def _():
            stage(5, 3)
            stage(4, 4)

        @pl.when(b == 1)
        def _():
            stage(5, 4)

        gate(1)

        @pl.when(b < 3)
        def _():
            stage(7, b + 1)

        @pl.when(b == 3)
        def _():
            stage(7, 4)

        gate(2)
        H[...] = H0[b]

        def step(t, u):
            h = H[...]
            low = h.astype(BF)

            def gates(p):
                rhs = jnp.concatenate([WD[b, p, q].reshape(512, 128) for q in range(4)], axis=1)
                return PRE[t, p] + dot(low, rhs)

            cand = jnp.tanh(sig(gates(0)) * gates(1))
            g = sig(gates(2) - 1.0)
            new = g * cand + (1.0 - g) * h
            H[...] = new
            ST[b, t] = (new * live_col).astype(BF)
            return u

        lax.fori_loop(0, STEPS, step, 0)
        pltpu.make_async_copy(ST.at[b], st_out.at[b], s_out.at[b]).start()

        @pl.when(b < 3)
        def _():
            ready(b + 1)

        return u

    lax.fori_loop(0, BLOCKS, compute, 0)
    wait_bytes(WP.at[:, :, :, 1 - c], d_rcv.at[8])
    out_p = pltpu.make_async_copy(WP, wp_out, s_out.at[4])
    out_p.start()
    wait_bytes(send.at[pl.ds(0, 127 * 16), :], s_snd.at[0])
    wait_bytes(send_z.at[pl.ds(0, 127)], s_snd.at[1])

    def drain(b, u):
        for s, W in enumerate((WS, WD)):
            wait_bytes(W.at[b, :, 0:2, 0, 0, 0], w_snd.at[b, s, 0])
            wait_bytes(W.at[b, :, 0:3, :, 0, 0], w_snd.at[b, s, 1])
            wait_bytes(W.at[b, :, 0:3, :, :, 0], w_snd.at[b, s, 2])
            wait_bytes(W.at[b, :, :, :, :, c], d_snd.at[2 * b + s])
        pltpu.make_async_copy(ST.at[b], st_out.at[b], s_out.at[b]).wait()
        return u

    lax.fori_loop(0, BLOCKS, drain, 0)
    for r in rings_p().values():
        for k in range(4):
            ref = r.part(r.at(0)) if k < 2 else r.half(r.at(-1 if k == 2 else 1), k - 2)
            r.make(ref, k).wait_send()
    wait_bytes(WP.at[:, :, :, c], d_snd.at[8])
    out_p.wait()


def prior_kernel(st, wp, live, samps_t, img, lp, stv, wpv, hot, scr, imgv, s_in, s_w, s_out):
    def part(s):
        return pl.ds(pl.multiple_of(s * 128, 128), 128)

    def get_w(b):
        return pltpu.make_async_copy(wp.at[:, b], wpv.at[:, b], s_w.at[b])

    def get_s(s):
        return pltpu.make_async_copy(st.at[:, :, part(s)], stv.at[:, :, part(s)], s_in.at[s])

    def put(s):
        return pltpu.make_async_copy(imgv.at[part(s)], img.at[part(s)], s_out.at[s])

    get_s(0).start()
    for b in range(BLOCKS):
        get_w(b).start()
    get_s(1).start()
    E = spread(32, 1024)
    cls = (lax.broadcasted_iota(jnp.int32, (256, 1024), 1) % 32).astype(F32)

    def hits(t, u):
        rep = dot(samps_t[t].astype(F32).astype(BF), E, ((0,), (0,)))
        hot[t] = jnp.where(rep == cls, 1.0, 0.0).astype(BF)
        return u

    lax.fori_loop(0, STEPS, hits, 0)

    def half(s, u):
        get_s(s).wait()

        def lay(b, u):
            for t in range(STEPS):
                scr[:, t, :] = stv[b, t, part(s)].astype(F32)
            cols = pl.ds(pl.multiple_of(b * 512, 512), 512)
            imgv[part(s), :, cols] = scr[...].astype(BF)
            return u

        lax.fori_loop(0, BLOCKS, lay, 0)
        put(s).start()

        @pl.when(s == 0)
        def _():
            for b in range(BLOCKS):
                get_w(b).wait()

        def step(t, u):
            low = jnp.concatenate([stv[b, t, part(s)] for b in range(BLOCKS)], axis=1)
            rhs = jnp.concatenate([wpv[j].reshape(2048, 128) for j in range(8)], axis=1)
            logits = dot(low, rhs)

            def grouped(v):
                hi = v.astype(BF)
                lo = (v - hi.astype(F32)).astype(BF)
                return dot(E, hi, ((1,), (1,))) + dot(E, lo, ((1,), (1,)))

            total = jnp.log(grouped(jnp.exp(logits)))
            hit = grouped(logits * hot[t, part(s)].astype(F32))
            lp[t, :, part(s)] = jnp.where(live[0:1, part(s)] > 0.0, hit - total, 0.0)
            return u

        lax.fori_loop(0, STEPS, step, 0)
        return u

    lax.fori_loop(0, 2, half, 0)
    put(0).wait()
    put(1).wait()


def on_device(deter, stoch, rows, counts, acts, samps, w_s, w_d, act, w_p):
    vmem = pl.BlockSpec(memory_space=pltpu.VMEM)
    hbm = pl.BlockSpec(memory_space=pl.ANY)
    dma = pltpu.SemaphoreType.DMA
    samps_t = samps.transpose(1, 2, 0)
    states, wp, live = pl.pallas_call(
        gru_kernel,
        name="gru",
        out_shape=(
            jax.ShapeDtypeStruct((4, 4, 256, 512), BF),
            jax.ShapeDtypeStruct((8, 4, 4, 2, 4, 16, 128), BF),
            jax.ShapeDtypeStruct((8, 256), F32),
        ),
        in_specs=[hbm] + [vmem] * 5 + [hbm, hbm, vmem, hbm],
        out_specs=(hbm, hbm, vmem),
        scratch_shapes=[
            pltpu.VMEM((256, 2048), F32),
            pltpu.VMEM((4, 3, 4, 4, 4, 2, 32, 128), BF),
            pltpu.VMEM((4, 3, 4, 4, 4, 2, 16, 128), BF),
            pltpu.VMEM((8, 4, 4, 2, 4, 16, 128), BF),
            pltpu.VMEM((2048, 128), jnp.int32),
            pltpu.VMEM((2048, 128), jnp.int32),
            pltpu.VMEM((128, 1, 128), jnp.int32),
            pltpu.VMEM((128, 1, 128), jnp.int32),
            pltpu.VMEM((256, 128), jnp.int32),
            pltpu.VMEM((4, 256, 512), F32),
            pltpu.VMEM((256, 512), F32),
            pltpu.VMEM((4, 256, 1024), BF),
            pltpu.VMEM((32, 6144), BF),
            pltpu.VMEM((4, 3, 256, 512), F32),
            pltpu.VMEM((4, 4, 256, 512), BF),
            dma((7,)), dma((2,)), dma((2,)),
            dma((4, 2, 3)), dma((4, 2, 8, 4)),
            dma((8, 4)), dma((8, 4)),
            dma((9,)), dma((9,)), dma((5,)),
        ],
        compiler_params=pltpu.CompilerParams(
            has_side_effects=True, vmem_limit_bytes=60 * 1024 * 1024
        ),
    )(deter, stoch.T, rows.T, counts, acts.T, samps_t, w_s, w_d, act, w_p)
    imagined, logp = pl.pallas_call(
        prior_kernel,
        name="prior",
        out_shape=(
            jax.ShapeDtypeStruct((256, 4, 2048), BF),
            jax.ShapeDtypeStruct((4, 32, 256), F32),
        ),
        in_specs=[hbm, hbm, vmem, vmem],
        out_specs=(hbm, vmem),
        scratch_shapes=[
            pltpu.VMEM((4, 4, 256, 512), BF),
            pltpu.VMEM((8, 4, 4, 2, 4, 16, 128), BF),
            pltpu.VMEM((4, 256, 1024), BF),
            pltpu.VMEM((128, 4, 512), F32),
            pltpu.VMEM((256, 4, 2048), BF),
            dma((2,)), dma((4,)), dma((2,)),
        ],
        compiler_params=pltpu.CompilerParams(vmem_limit_bytes=60 * 1024 * 1024),
    )(states, wp, live, samps_t)
    return (imagined, logp.transpose(2, 0, 1))


def solution(mesh):
    in_specs = (
        P(("gx", "gy"), None),
        P(("gx", "gy"), None),
        P(("gx", "gy"), None),
        P(("gx", "gy"), None),
        P(("gx", "gy"), None),
        P(("gx", "gy"), None, None),
        P("gy", None),
        P(None, "gy", None),
        P(),
        P("gy", None),
    )
    out_specs = (P(("gx", "gy"), None, None), P(("gx", "gy"), None, None))
    return jax.shard_map(
        on_device, mesh=mesh, in_specs=in_specs, out_specs=out_specs, check_vma=False
    )
```

time: 147 us -> 127 us (0.86); the launches traced: 146 us -> 124 us
  local copies, waits for them, and re-layouts: 18.9 us -> 0 us
  Pallas kernels: 126 us -> 123 us
    unnamed x7 -> x0, local copies, waits for them, and re-layouts: 11.6 us -> none
    pallas_call x1, Pallas kernels: 115 us -> 108 us  [on_device(): pl.pallas_call(gru_kernel, name='gru', out_shape=(jax.ShapeDtypeStruct((4...]
    transpose x1 -> x0, local copies, waits for them, and re-layouts: 7.3 us -> none  [on_device(): imagined = states.transpose(2, 1, 0, 3).reshape(256, 4, 2048)]
    pallas_call x1, Pallas kernels: 11 us -> 15.8 us  [on_device(): pl.pallas_call(prior_kernel, name='prior', out_shape=(jax.ShapeDtypeStruc...]
where the time goes in v1:
time: 127 us; the launch traced here: 124 us
  Pallas kernels  123 us (97%)
    pallas_call x1, Pallas kernels, on_device(): pl.pallas_call(gru_kernel, name='gru', out_shape=(jax.ShapeDtypeStruct((4...  108 us
    pallas_call x1, Pallas kernels, on_device(): pl.pallas_call(prior_kernel, name='prior', out_shape=(jax.ShapeDtypeStruc...  15.8 us

profile of v1, /device:TPU:1, one launch (start us, length us, event | category | flops | bytes accessed | tf_op | source)
XLA Modules:
  0.0 124.1 jit_solution(7593224042304554713)
XLA Ops:
  0.6 107.7 %gru.1 = (bf16[4,4,256,512]{3,2,1,0:T(8,128)(2,1)}, bf16[8,4,4,2,4,16,128]{6,5,4,3,2,1,0:T(8,128)(2,1)}, f32[8,256]{1,0:T(8,128)}) custom-call(f32[256,2048]{1,0:T(8,128)} %deter_h.1, s32[32,256]{1,0:T(8,128)} %bitcast.7, s32[2,128]{1,0:T(2,128)} %bitcast.9, s32[1,128]{1,0:T(1,128)} %counts.1, s32[4,256]{1,0:T(4,128)} %bitcast.8, s32[4,32,256]{2,1,0:T(8,128)} %bitcast.5, ...), custom_call_target="tpu_custom_call" | custom-call | tf_op jit(solution)/shard_map/gru/pallas_call | solution.py:496
  108.3 15.8 %prior.1 = (bf16[256,4,2048]{2,1,0:T(4,128)(2,1)}, f32[4,32,256]{2,1,0:T(8,128)}) custom-call(bf16[4,4,256,512]{3,2,1,0:T(8,128)(2,1)} %get-tuple-element.7.st, bf16[8,4,4,2,4,16,128]{6,5,4,3,2,1,0:T(8,128)(2,1)} %get-tuple-element.8.wp, f32[8,256]{1,0:T(8,128)} %get-tuple-element.9.live, s32[4,32,256]{2,1,0:T(8,128)} %bitcast.6), custom_call_target="tpu_custom_call" | custom-call | tf_op jit(solution)/shard_map/prior/pallas_call | solution.py:531

commit v2 on v1

v2 whole, which is shorter than its diff:
```python
import functools

import jax
import jax.numpy as jnp
from jax import lax
from jax.experimental import pallas as pl
from jax.experimental.pallas import tpu as pltpu
from jax.sharding import PartitionSpec as P

STEPS = 4
BLOCKS = 4
BF = jnp.bfloat16
F32 = jnp.float32
MESH = pl.DeviceIdType.MESH
SCALE = 32767.0


def dot(a, b, dims=((1,), (0,))):
    return lax.dot_general(a, b, (dims, ((), ())), preferred_element_type=F32)


def spread(rows, lanes):
    g = lax.broadcasted_iota(jnp.int32, (rows, lanes), 0)
    k = lax.broadcasted_iota(jnp.int32, (rows, lanes), 1)
    return jnp.where((k >= g * 32) & (k < g * 32 + 32), 1.0, 0.0).astype(BF)


def sig(v):
    return 0.5 * jnp.tanh(0.5 * v) + 0.5


def gru_kernel(
    deter_h, stoch_t, rows_t, counts, acts_t, samps_t, w_s, w_d, act, w_p,
    st_out, wp_out, live_out,
    deter, WS, WD, WP, send, recv, send_z, recv_z, zf, H0, H, OH, ACT, AH, PRE, ST,
    s_loc, s_snd, s_rcv, w_snd, w_rcv, p_snd, p_rcv, d_snd, d_rcv, s_out,
):
    x = lax.axis_index("gx")
    gy = lax.axis_index("gy")
    y, z, c = gy // 8, (gy // 2) % 4, gy % 2
    me = x * 32 + gy

    def dev(tx, ty, tz, tc):
        return (tx, ty * 8 + tz * 2 + tc)

    def near(dim, step):
        s = (step + 4) % 4
        if dim == "x":
            return dev((x + s) % 4, y, z, c)
        if dim == "y":
            return dev(x, (y + s) % 4, z, c)
        return dev(x, y, (z + s) % 4, c)

    pos = {"x": x, "y": y, "z": z}
    partner = dev(x, y, z, 1 - c)

    def wait_bytes(ref, sem):
        pltpu.make_async_copy(ref, ref, sem).wait()

    barrier = pltpu.get_barrier_semaphore()

    xs, ys, zs = ([(v + i) % 4 for i in range(4)] for v in (x, y, z))
    y8, z2, cs = [v * 8 for v in ys], [v * 2 for v in zs], [c, 1 - c]

    def peers(*dxs):
        for dx in dxs:
            for dy in range(4):
                for dz in range(4):
                    for dc in range(2):
                        if dx + dy + dz + dc > 0:
                            g = y8[dy] + (z2[dz] + cs[dc])
                            yield (xs[dx], g), xs[dx] * 32 + g

    for to, _ in peers(0, 1, 2, 3):
        pl.semaphore_signal(barrier, inc=1, device_id=to, device_id_type=MESH)
    get_deter = pltpu.make_async_copy(deter_h, deter, s_loc.at[6])

    def fill(b, u):
        for p in range(3):
            for q in range(4) if p == 0 else (x,):
                col = pl.multiple_of(b * 1536 + p * 512 + q * 128, 128)
                pltpu.make_async_copy(
                    w_s.at[:, pl.ds(col, 128)], WS.at[b, p, q, y, z, c], s_loc.at[0]
                ).start()
                col = pl.multiple_of(p * 512 + q * 128, 128)
                pltpu.make_async_copy(
                    w_d.at[b, :, pl.ds(col, 128)], WD.at[b, p, q, y, z, c], s_loc.at[1]
                ).start()
        return u

    lax.fori_loop(0, 4, fill, 0)
    for j in range(8):
        if j < 3:
            for q in range(4):
                pltpu.make_async_copy(
                    w_p.at[pl.ds(q * 16, 16), pl.ds(j * 128, 128)], WP.at[j, y, z, c, q], s_loc.at[2]
                ).start()
        else:
            pltpu.make_async_copy(
                w_p.at[pl.ds(pl.multiple_of(x * 16, 16), 16), pl.ds(j * 128, 128)],
                WP.at[j, y, z, c, x],
                s_loc.at[3],
            ).start()
    get_deter.start()

    iota = lax.broadcasted_iota(jnp.int32, (256, 128), 0)
    sel_t = jnp.concatenate(
        [jnp.where(iota == rows_t[i : i + 1, :], 1.0, 0.0) for i in range(2)], axis=1
    )
    sel = jnp.transpose(sel_t).astype(BF)
    picked = dot(stoch_t[...].astype(F32).astype(BF), sel_t.astype(BF))
    zv = [
        jnp.where(counts[...] > i, picked[:, 128 * i : 128 * i + 128], 64.0) for i in range(2)
    ]
    zv = jnp.concatenate(zv + [jnp.zeros((64, 128), F32)], axis=0)
    send_z[...] = jnp.transpose(zv).astype(jnp.int32).reshape(128, 1, 128)

    wait_bytes(WS.at[0, :, :, 0:2, 0, 0], s_loc.at[0])
    wait_bytes(WD.at[0, :, :, 0:2, 0, 0], s_loc.at[1])
    wait_bytes(WP.at[0:3, 0, 0, 0], s_loc.at[2])
    wait_bytes(WP.at[0:5, 0, 0, 0, 0], s_loc.at[3])

    pl.semaphore_wait(barrier, 127)

    def copy_to(ref, snd, rcv, to):
        return pltpu.make_async_remote_copy(
            src_ref=ref, dst_ref=ref, send_sem=snd, recv_sem=rcv, device_id=to, device_id_type=MESH
        )

    class Ring:
        def __init__(self, dim, sets, snd, rcv, sides, far):
            self.dim, self.sets, self.snd, self.rcv = dim, sets, snd, rcv
            self.sides, self.far = sides, far

        def at(self, step):
            return (pos[self.dim] + step + 4) % 4

        def send(self, ref, k, stage):
            copy_to(ref, self.snd, self.rcv.at[stage], near(self.dim, 1 if k == 0 else -1)).start()

        def start(self, hand):
            for part, half in self.sets:
                for k in range(2):
                    self.send(part(self.at(0)), k, 0)
            if hand:
                for part, half in self.sets:
                    hand(part(self.at(0)))

        def mid(self, hand):
            wait_bytes(self.sides, self.rcv.at[0])
            for part, half in self.sets:
                for k in range(2):
                    ref = half(self.at(-1 if k == 0 else 1), k)
                    if ref is not None:
                        self.send(ref, k, 1)
            if hand:
                for part, half in self.sets:
                    for k in (-1, 1):
                        hand(part(self.at(k)))

        def end(self, hand):
            wait_bytes(self.far, self.rcv.at[1])
            if hand:
                for part, half in self.sets:
                    hand(part(self.at(2)))

    hs = (slice(0, 2), slice(2, 4))

    def rings(b):
        def ring(n, dim, part, half, group, size):
            sets = [(functools.partial(part, W), functools.partial(half, W)) for W in (WS, WD)]
            spare = {1: (0, 0, 0), 4: (slice(None), 0, 0), 16: (slice(None), slice(None), 0)}[size]
            return Ring(
                dim, sets, w_snd.at[b, group], w_rcv.at[b, n],
                WD.at[(slice(0, 2), slice(0, 3)) + spare + (0,)], WD.at[(0, slice(0, 3)) + spare + (0,)],
            )

        def split(W, ref, h):
            if W is WS:
                return ref.at[pl.ds(16 * h, 16)]
            return ref if h == 0 else None

        return {
            "ay": ring(0, "y", lambda W, i: W.at[b, 0, :, i, z, c], lambda W, i, h: W.at[b, 0, hs[h], i, z, c], 1, 4),
            "by": ring(1, "y", lambda W, i: W.at[b, 1, x, i, z, c], lambda W, i, h: split(W, W.at[b, 1, x, i, z, c], h), 0, 1),
            "cz": ring(2, "z", lambda W, i: W.at[b, 2, x, y, i, c], lambda W, i, h: split(W, W.at[b, 2, x, y, i, c], h), 0, 1),
            "bz": ring(3, "z", lambda W, i: W.at[b, 1, x, :, i, c], lambda W, i, h: W.at[b, 1, x, hs[h], i, c], 1, 4),
            "cx": ring(4, "x", lambda W, i: W.at[b, 2, i, y, :, c], lambda W, i, h: W.at[b, 2, i, y, hs[h], c], 1, 4),
            "fz": ring(5, "z", lambda W, i: W.at[b, 0, :, :, i, c], lambda W, i, h: W.at[b, 0, hs[h], :, i, c], 2, 16),
            "fx": ring(6, "x", lambda W, i: W.at[b, 1, i, :, :, c], lambda W, i, h: W.at[b, 1, i, hs[h], :, c], 2, 16),
            "fy": ring(7, "y", lambda W, i: W.at[b, 2, :, i, :, c], lambda W, i, h: W.at[b, 2, hs[h], i, :, c], 2, 16),
        }

    def rings_p():
        def ring(n, dim, part, half, group, sides, far):
            return Ring(dim, [(part, half)], p_snd.at[group], p_rcv.at[n], sides, far)

        return {
            "ay": ring(0, "y", lambda i: WP.at[0:3, i, z, c], lambda i, h: WP.at[0:3, i, z, c, hs[h]], 0, WP.at[0:3, :, 0, :, 0], WP.at[0:3, :, 0, 0, 0]),
            "by": ring(1, "y", lambda i: WP.at[3:6, i, z, c, x], lambda i, h: WP.at[3 + h : 4 + 2 * h, i, z, c, x], 1, WP.at[0:6, 0, 0, 0, 0], WP.at[0:3, 0, 0, 0, 0]),
            "cz": ring(2, "z", lambda i: WP.at[6:8, y, i, c, x], lambda i, h: WP.at[6 + h : 7 + h, y, i, c, x], 1, WP.at[0:4, 0, 0, 0, 0], WP.at[0:2, 0, 0, 0, 0]),
            "bz": ring(3, "z", lambda i: WP.at[3:6, :, i, c, x], lambda i, h: WP.at[3:6, hs[h], i, c, x], 0, WP.at[0:3, :, 0, :, 0], WP.at[0:3, :, 0, 0, 0]),
            "cx": ring(4, "x", lambda i: WP.at[6:8, y, :, c, i], lambda i, h: WP.at[6:8, y, hs[h], c, i], 2, WP.at[0:4, :, 0, 0, 0], WP.at[0:2, :, 0, 0, 0]),
            "fz": ring(5, "z", lambda i: WP.at[0:3, :, i, c], lambda i, h: WP.at[0:3, hs[h], i, c], 3, WP.at[0:3, :, :, :, 0], WP.at[0:3, :, :, 0, 0]),
            "fx": ring(6, "x", lambda i: WP.at[3:6, :, :, c, i], lambda i, h: WP.at[3:6, hs[h], :, c, i], 3, WP.at[0:3, :, :, :, 0], WP.at[0:3, :, :, 0, 0]),
            "fy": ring(7, "y", lambda i: WP.at[6:8, i, :, c], lambda i, h: WP.at[6:8, i, hs[h], c], 4, WP.at[0:2, :, :, :, 0], WP.at[0:2, :, :, 0, 0]),
        }

    def over(k):
        def go(ref):
            copy_to(ref, d_snd.at[k], d_rcv.at[k], partner).start()

        return go

    def stage(n, b):
        if isinstance(b, int) and b == 4:
            r, give = rings_p(), over(4)
        else:
            r, give = rings(b), over(b)

        def each(names, what, hand=None):
            for name in names:
                what(r[name], hand)

        if n == 1:
            each(("by", "cz", "ay"), Ring.start)
        elif n == 2:
            each(("by", "cz", "ay"), Ring.mid)
        elif n == 3:
            each(("by", "cz"), Ring.end)
            each(("bz", "cx"), Ring.start)
        elif n == 4:
            each(("bz", "cx"), Ring.mid)
            each(("ay",), Ring.end)
        elif n == 5:
            each(("bz", "cx"), Ring.end)
            each(("fz", "fx", "fy"), Ring.start, give)
        elif n == 6:
            each(("fz", "fx", "fy"), Ring.mid, give)
        else:
            each(("fz", "fx", "fy"), Ring.end, give)

    def ready(b):
        wait_bytes(WD.at[0:3, :, :, :, :, 0], d_rcv.at[b])

    stage(1, 0)
    stage(1, 1)
    for to, n in peers(0, 1, 2, 3):
        pltpu.make_async_remote_copy(
            src_ref=send_z.at[n], dst_ref=recv_z.at[me],
            send_sem=s_snd.at[1], recv_sem=s_rcv.at[1], device_id=to, device_id_type=MESH,
        ).start()

    get_deter.wait()
    for k in range(8):
        lo = 512 * (k // 2) + 128 * (k % 2)
        parts = []
        for col in (lo, lo + 256):
            code = jnp.round(deter[:, col : col + 128] * SCALE)
            high = jnp.floor(code * (1.0 / 256.0))
            parts += [high.astype(BF), (code - high * 256.0).astype(BF)]
        got = dot(sel, jnp.concatenate(parts, axis=1))
        v0 = (got[:, 0:128] * 256.0 + got[:, 128:256]).astype(jnp.int32)
        v1 = (got[:, 256:384] * 256.0 + got[:, 384:512]).astype(jnp.int32)
        word = v1 * 65536 + (v0 + 32768)
        send[pl.ds(k, 128, stride=16), :] = word[0:128]
        send[pl.ds(8 + k, 128, stride=16), :] = word[128:256]
        if k == 2:
            stage(2, 0)

    def rows_of(n):
        return pl.ds(pl.multiple_of(n * 16, 16), 16)

    def send_rows(dx):
        for to, n in peers(dx):
            pltpu.make_async_remote_copy(
                src_ref=send.at[rows_of(n), :], dst_ref=recv.at[rows_of(me), :],
                send_sem=s_snd.at[0], recv_sem=s_rcv.at[0], device_id=to, device_id_type=MESH,
            ).start()

    stage(3, 0)
    send_rows(0)
    stage(2, 1)
    stage(1, 2)
    own = [
        pltpu.make_async_copy(send.at[rows_of(me), :], recv.at[rows_of(me), :], s_loc.at[4]),
        pltpu.make_async_copy(send_z.at[me], recv_z.at[me], s_loc.at[5]),
    ]
    for cp in own:
        cp.start()

    E = spread(32, 1024)
    cls = (lax.broadcasted_iota(jnp.int32, (256, 1024), 1) % 32).astype(F32)

    def one_hot(t):
        rep = dot(samps_t[t - 1].astype(F32).astype(BF), E, ((0,), (0,)))
        OH[256 * t : 256 * t + 256, :] = jnp.where(rep == cls, 1.0, 0.0).astype(BF)

    def act_terms(b):
        def piece(n, u):
            p, e = n // 2, n % 2
            cols = pl.ds(pl.multiple_of(b * 1536 + n * 256, 256), 256)
            PRE[b, p, :, pl.ds(pl.multiple_of(e * 256, 256), 256)] = dot(AH[...], ACT[:, cols])
            return u

        lax.fori_loop(0, 6, piece, 0)

    one_hot(1)
    one_hot(2)
    stage(4, 0)
    stage(3, 1)
    send_rows(1)
    stage(2, 2)
    one_hot(3)
    ACT[...] = jnp.zeros_like(ACT)
    ACT[0 : act.shape[0], :] = act[...]
    which = lax.broadcasted_iota(jnp.int32, (32, 256), 0)
    for t in range(STEPS):
        a_hot = jnp.where(which == acts_t[t : t + 1, :], 1.0, 0.0)
        AH[256 * t : 256 * t + 256, :] = jnp.transpose(a_hot).astype(BF)
    stage(5, 0)
    stage(1, 3)
    act_terms(0)
    stage(4, 1)
    stage(3, 2)
    send_rows(2)
    act_terms(1)
    act_terms(2)
    act_terms(3)
    stage(6, 0)
    send_rows(3)
    stage(5, 1)
    stage(2, 3)

    wait_bytes(recv_z.at[pl.ds(0, 127)], s_rcv.at[1])
    own[1].wait()
    zv = recv_z[...].reshape(128, 128)
    zf[pl.ds(0, 128, stride=2), :] = zv
    zf[pl.ds(1, 128, stride=2), :] = pltpu.roll(zv, 96, 1)
    codes = zf[...].astype(F32)
    rep = dot(codes[:, 0:32].astype(BF), E)
    OH[0:256, :] = jnp.where(rep == cls, 1.0, 0.0).astype(BF)
    alive = jnp.where(codes < 32.0, 1.0, 0.0)
    lane0 = jnp.where(lax.broadcasted_iota(jnp.int32, (8, 128), 1) == 0, 1.0, 0.0).astype(BF)
    live_out[...] = dot(lane0, alive.astype(BF), ((1,), (1,)))
    live_col = alive[:, 0:1]
    stage(7, 0)
    ready(0)

    def start_rows():
        wait_bytes(recv.at[pl.ds(0, 127 * 16), :], s_rcv.at[0])
        own[0].wait()
        for k in range(8):
            word = recv[pl.ds(k, 256, stride=8), :]
            v1 = lax.shift_right_arithmetic(word, 16)
            v0 = (word & 65535) - 32768
            b, e = k // 2, (k % 2) * 128
            H0[b, :, e : e + 128] = v0.astype(F32) * (1.0 / SCALE)
            H0[b, :, 256 + e : 384 + e] = v1.astype(F32) * (1.0 / SCALE)

    def put_states(b):
        return pltpu.make_async_copy(ST.at[b % 2], st_out.at[b], s_out.at[b])

    def compute(b, u):
        def gate(p):
            def piece(e, u):
                rhs = jnp.concatenate(
                    [WS[b, p, 2 * e + i].reshape(1024, 128) for i in range(2)], axis=1
                )
                cols = pl.ds(pl.multiple_of(e * 256, 256), 256)
                PRE[b, p, :, cols] = PRE[b, p, :, cols] + dot(OH[...], rhs)
                return u

            lax.fori_loop(0, 2, piece, 0)

        def also(plan):
            for when, stages in plan.items():

                @pl.when(b == when)
                def _():
                    for n, k in stages:
                        stage(n, k)

        gate(0)
        also({0: ((4, 2), (1, 4)), 1: ((6, 2), (3, 4)), 2: ((6, 3),), 3: ((6, 4),)})
        gate(1)
        also({0: ((6, 1), (3, 3)), 1: ((5, 3),), 2: ((5, 4),)})
        gate(2)

        @pl.when(b == 0)
        def _():
            stage(5, 2)
            start_rows()

        H[...] = H0[b]

        @pl.when(b >= 2)
        def _():
            put_states(b - 2).wait()

        def step(t, u):
            h = H[...]
            low = h.astype(BF)
            rows = pl.ds(pl.multiple_of(t * 256, 256), 256)

            def gates(p):
                rhs = jnp.concatenate([WD[b, p, q].reshape(512, 128) for q in range(4)], axis=1)
                return PRE[b, p, rows, :] + dot(low, rhs)

            cand = jnp.tanh(sig(gates(0)) * gates(1))
            g = sig(gates(2) - 1.0)
            new = g * cand + (1.0 - g) * h
            H[...] = new
            ST[b % 2, t] = (new * live_col).astype(BF)
            return u

        lax.fori_loop(0, 2, step, 0)

        @pl.when(b < 3)
        def _():
            stage(7, b + 1)

        also({0: ((2, 4),), 3: ((7, 4),)})
        lax.fori_loop(2, STEPS, step, 0)
        put_states(b).start()

        also({0: ((4, 3),), 1: ((4, 4),)})

        @pl.when(b < 3)
        def _():
            ready(b + 1)

        return u

    lax.fori_loop(0, BLOCKS, compute, 0)
    wait_bytes(WP.at[:, :, :, 0], d_rcv.at[4])
    out_p = pltpu.make_async_copy(WP, wp_out, s_out.at[4])
    out_p.start()
    wait_bytes(send.at[pl.ds(0, 127 * 16), :], s_snd.at[0])
    wait_bytes(send_z.at[pl.ds(0, 127)], s_snd.at[1])

    def drain(b, u):
        wait_bytes(WD.at[0, :, 0:3, 0:2, 0, 0], w_snd.at[b, 0])
        wait_bytes(WD.at[0, :, 0:3, 0:3, :, 0], w_snd.at[b, 1])
        wait_bytes(WD.at[0:2, :, 0:3, :, 0:3, :], w_snd.at[b, 2])
        wait_bytes(WD.at[0:3, :, :, :, :, 0], d_snd.at[b])

        @pl.when(b >= 2)
        def _():
            put_states(b).wait()

        return u

    lax.fori_loop(0, BLOCKS, drain, 0)
    wait_bytes(WP.at[0:3, :, 0:3, :, 0], p_snd.at[0])
    wait_bytes(WP.at[0:5, 0:3, 0, 0, 0], p_snd.at[1])
    wait_bytes(WP.at[0:3, :, 0, :, 0], p_snd.at[2])
    wait_bytes(WP.at[0:3, :, :, :, 0:3], p_snd.at[3])
    wait_bytes(WP.at[0:3, :, :, :, 0], p_snd.at[4])
    wait_bytes(WP.at[:, :, :, 0], d_snd.at[4])
    out_p.wait()


def prior_kernel(st, wp, live, samps_t, img, lp, stv, wpv, hot, scr, imgv, s_in, s_w, s_out):
    def part(s):
        return pl.ds(pl.multiple_of(s * 128, 128), 128)

    def get_w(n):
        return pltpu.make_async_copy(wp.at[pl.ds(2 * n, 2)], wpv.at[pl.ds(2 * n, 2)], s_w.at[n])

    def get_s(s):
        return pltpu.make_async_copy(st.at[:, :, part(s)], stv.at[:, :, part(s)], s_in.at[s])

    def put(s):
        return pltpu.make_async_copy(imgv.at[part(s)], img.at[part(s)], s_out.at[s])

    get_s(0).start()
    for n in range(4):
        get_w(n).start()
    get_s(1).start()
    E = spread(32, 1024)
    E8 = spread(8, 256)
    cls = (lax.broadcasted_iota(jnp.int32, (256, 1024), 1) % 32).astype(F32)

    def hits(t, u):
        rep = dot(samps_t[t].astype(F32).astype(BF), E, ((0,), (0,)))
        hot[t] = jnp.where(rep == cls, 1.0, 0.0).astype(BF)
        return u

    lax.fori_loop(0, STEPS, hits, 0)

    def half(s, u):
        get_s(s).wait()

        def columns(n, u):
            @pl.when(s == 0)
            def _():
                get_w(n).wait()

            low = jnp.concatenate([stv[b, :, part(s)].reshape(512, 512) for b in range(BLOCKS)], axis=1)
            rhs = jnp.concatenate([wpv[2 * n + i].reshape(2048, 128) for i in range(2)], axis=1)
            logits = dot(low, rhs)
            for t in range(STEPS):
                scr[:, t, :] = stv[n, t, part(s)].astype(F32)
            imgv[part(s), :, pl.ds(pl.multiple_of(n * 512, 512), 512)] = scr[...].astype(BF)

            def grouped(v):
                hi = v.astype(BF)
                lo = (v - hi.astype(F32)).astype(BF)
                return dot(E8, hi, ((1,), (1,))) + dot(E8, lo, ((1,), (1,)))

            cols = pl.ds(pl.multiple_of(n * 256, 256), 256)
            total = jnp.log(grouped(jnp.exp(logits)))
            hit = grouped(logits * hot[:, part(s), cols].reshape(512, 256).astype(F32))
            value = hit - total
            for t in range(STEPS):
                lp[t, pl.ds(pl.multiple_of(n * 8, 8), 8), part(s)] = jnp.where(
                    live[:, part(s)] > 0.0, value[:, 128 * t : 128 * t + 128], 0.0
                )
            return u

        lax.fori_loop(0, 4, columns, 0)
        put(s).start()
        return u

    lax.fori_loop(0, 2, half, 0)
    put(0).wait()
    put(1).wait()


def on_device(deter, stoch, rows, counts, acts, samps, w_s, w_d, act, w_p):
    vmem = pl.BlockSpec(memory_space=pltpu.VMEM)
    hbm = pl.BlockSpec(memory_space=pl.ANY)
    dma = pltpu.SemaphoreType.DMA
    samps_t = samps.transpose(1, 2, 0)
    states, wp, live = pl.pallas_call(
        gru_kernel,
        name="gru",
        out_shape=(
            jax.ShapeDtypeStruct((4, 4, 256, 512), BF),
            jax.ShapeDtypeStruct((8, 4, 4, 2, 4, 16, 128), BF),
            jax.ShapeDtypeStruct((8, 256), F32),
        ),
        in_specs=[hbm] + [vmem] * 5 + [hbm, hbm, vmem, hbm],
        out_specs=(hbm, hbm, vmem),
        scratch_shapes=[
            pltpu.VMEM((256, 2048), F32),
            pltpu.VMEM((4, 3, 4, 4, 4, 2, 32, 128), BF),
            pltpu.VMEM((4, 3, 4, 4, 4, 2, 16, 128), BF),
            pltpu.VMEM((8, 4, 4, 2, 4, 16, 128), BF),
            pltpu.VMEM((2048, 128), jnp.int32),
            pltpu.VMEM((2048, 128), jnp.int32),
            pltpu.VMEM((128, 1, 128), jnp.int32),
            pltpu.VMEM((128, 1, 128), jnp.int32),
            pltpu.VMEM((256, 128), jnp.int32),
            pltpu.VMEM((4, 256, 512), F32),
            pltpu.VMEM((256, 512), F32),
            pltpu.VMEM((1024, 1024), BF),
            pltpu.VMEM((32, 6144), BF),
            pltpu.VMEM((1024, 32), BF),
            pltpu.VMEM((4, 3, 1024, 512), F32),
            pltpu.VMEM((2, 4, 256, 512), BF),
            dma((7,)), dma((2,)), dma((2,)),
            dma((4, 3)), dma((4, 8, 2)),
            dma((5,)), dma((8, 2)),
            dma((5,)), dma((5,)), dma((5,)),
        ],
        compiler_params=pltpu.CompilerParams(
            collective_id=0, has_side_effects=True, vmem_limit_bytes=63 * 1024 * 1024
        ),
    )(deter, stoch.T, rows.T, counts, acts.T, samps_t, w_s, w_d, act, w_p)
    imagined, logp = pl.pallas_call(
        prior_kernel,
        name="prior",
        out_shape=(
            jax.ShapeDtypeStruct((256, 4, 2048), BF),
            jax.ShapeDtypeStruct((4, 32, 256), F32),
        ),
        in_specs=[hbm, hbm, vmem, vmem],
        out_specs=(hbm, vmem),
        scratch_shapes=[
            pltpu.VMEM((4, 4, 256, 512), BF),
            pltpu.VMEM((8, 4, 4, 2, 4, 16, 128), BF),
            pltpu.VMEM((4, 256, 1024), BF),
            pltpu.VMEM((128, 4, 512), F32),
            pltpu.VMEM((256, 4, 2048), BF),
            dma((2,)), dma((4,)), dma((2,)),
        ],
        compiler_params=pltpu.CompilerParams(vmem_limit_bytes=60 * 1024 * 1024),
    )(states, wp, live, samps_t)
    return (imagined, logp.transpose(2, 0, 1))


def solution(mesh):
    in_specs = (
        P(("gx", "gy"), None),
        P(("gx", "gy"), None),
        P(("gx", "gy"), None),
        P(("gx", "gy"), None),
        P(("gx", "gy"), None),
        P(("gx", "gy"), None, None),
        P("gy", None),
        P(None, "gy", None),
        P(),
        P("gy", None),
    )
    out_specs = (P(("gx", "gy"), None, None), P(("gx", "gy"), None, None))
    return jax.shard_map(
        on_device, mesh=mesh, in_specs=in_specs, out_specs=out_specs, check_vma=False
    )
```

time: 127 us -> 106 us (0.83); the launches traced: 124 us -> 106 us
  Pallas kernels: 123 us -> 105 us
    pallas_call x1, Pallas kernels: 108 us -> 88.3 us  [on_device(): pl.pallas_call(gru_kernel, name='gru', out_shape=(jax.ShapeDtypeStruct((4...]
where the time goes in v2:
time: 106 us
  Pallas kernels  105 us (99%)
    pallas_call x1, Pallas kernels, on_device(): pl.pallas_call(gru_kernel, name='gru', out_shape=(jax.ShapeDtypeStruct((4...  88.3 us
    pallas_call x1, Pallas kernels, on_device(): pl.pallas_call(prior_kernel, name='prior', out_shape=(jax.ShapeDtypeStruc...  16.9 us

profile of v2, /device:TPU:1, one launch (start us, length us, event | category | flops | bytes accessed | tf_op | source)
XLA Modules:
  0.0 105.9 jit_solution(5804167765576603511)
XLA Ops:
  0.6 88.3 %gru.1 = (bf16[4,4,256,512]{3,2,1,0:T(8,128)(2,1)}, bf16[8,4,4,2,4,16,128]{6,5,4,3,2,1,0:T(8,128)(2,1)}, f32[8,256]{1,0:T(8,128)}) custom-call(f32[256,2048]{1,0:T(8,128)} %deter_h.1, s32[32,256]{1,0:T(8,128)} %bitcast.7, s32[2,128]{1,0:T(2,128)} %bitcast.9, s32[1,128]{1,0:T(1,128)} %counts.1, s32[4,256]{1,0:T(4,128)} %bitcast.8, s32[4,32,256]{2,1,0:T(8,128)} %bitcast.5, ...), custom_call_target="tpu_custom_call" | custom-call | tf_op jit(solution)/shard_map/gru/pallas_call | solution.py:536
  89.0 16.9 %prior.1 = (bf16[256,4,2048]{2,1,0:T(4,128)(2,1)}, f32[4,32,256]{2,1,0:T(8,128)}) custom-call(bf16[4,4,256,512]{3,2,1,0:T(8,128)(2,1)} %get-tuple-element.7.st, bf16[8,4,4,2,4,16,128]{6,5,4,3,2,1,0:T(8,128)(2,1)} %get-tuple-element.8.wp, f32[8,256]{1,0:T(8,128)} %get-tuple-element.9.live, s32[4,32,256]{2,1,0:T(8,128)} %bitcast.6), custom_call_target="tpu_custom_call" | custom-call | tf_op jit(solution)/shard_map/prior/pallas_call | solution.py:572

commit v3 on v2

--- a/solution.py
+++ b/solution.py
@@ -62,16 +62,16 @@
     xs, ys, zs = ([(v + i) % 4 for i in range(4)] for v in (x, y, z))
     y8, z2, cs = [v * 8 for v in ys], [v * 2 for v in zs], [c, 1 - c]
 
-    def peers(*dxs):
-        for dx in dxs:
+    def peers(*groups):
+        for dx in range(4):
             for dy in range(4):
                 for dz in range(4):
                     for dc in range(2):
-                        if dx + dy + dz + dc > 0:
+                        if dx + dy + dz + dc > 0 and (dx + dy + dz) % 4 in groups:
                             g = y8[dy] + (z2[dz] + cs[dc])
                             yield (xs[dx], g), xs[dx] * 32 + g
 
-    for to, _ in peers(0, 1, 2, 3):
+    for to, _ in reversed(list(peers(0, 1, 2, 3))):
         pl.semaphore_signal(barrier, inc=1, device_id=to, device_id_type=MESH)
     get_deter = pltpu.make_async_copy(deter_h, deter, s_loc.at[6])
 
@@ -271,8 +271,8 @@
     def rows_of(n):
         return pl.ds(pl.multiple_of(n * 16, 16), 16)
 
-    def send_rows(dx):
-        for to, n in peers(dx):
+    def send_rows(group):
+        for to, n in peers(group):
             pltpu.make_async_remote_copy(
                 src_ref=send.at[rows_of(n), :], dst_ref=recv.at[rows_of(me), :],
                 send_sem=s_snd.at[0], recv_sem=s_rcv.at[0], device_id=to, device_id_type=MESH,
@@ -328,8 +328,8 @@
     act_terms(2)
     act_terms(3)
     stage(6, 0)
+    stage(5, 1)
     send_rows(3)
-    stage(5, 1)
     stage(2, 3)
 
     wait_bytes(recv_z.at[pl.ds(0, 127)], s_rcv.at[1])
@@ -358,6 +358,9 @@
             H0[b, :, e : e + 128] = v0.astype(F32) * (1.0 / SCALE)
             H0[b, :, 256 + e : 384 + e] = v1.astype(F32) * (1.0 / SCALE)
 
+    def put_prior(e, k):
+        return pltpu.make_async_copy(WP.at[:, :, :, e], wp_out.at[:, :, :, e], s_out.at[k])
+
     def put_states(b):
         return pltpu.make_async_copy(ST.at[b % 2], st_out.at[b], s_out.at[b])
 
@@ -421,6 +424,11 @@
             stage(7, b + 1)
 
         also({0: ((2, 4),), 3: ((7, 4),)})
+
+        @pl.when(b == 3)
+        def _():
+            put_prior(c, 4).start()
+
         lax.fori_loop(2, STEPS, step, 0)
         put_states(b).start()
 
@@ -434,8 +442,7 @@
 
     lax.fori_loop(0, BLOCKS, compute, 0)
     wait_bytes(WP.at[:, :, :, 0], d_rcv.at[4])
-    out_p = pltpu.make_async_copy(WP, wp_out, s_out.at[4])
-    out_p.start()
+    put_prior(1 - c, 5).start()
     wait_bytes(send.at[pl.ds(0, 127 * 16), :], s_snd.at[0])
     wait_bytes(send_z.at[pl.ds(0, 127)], s_snd.at[1])
 
@@ -458,10 +465,11 @@
     wait_bytes(WP.at[0:3, :, :, :, 0:3], p_snd.at[3])
     wait_bytes(WP.at[0:3, :, :, :, 0], p_snd.at[4])
     wait_bytes(WP.at[:, :, :, 0], d_snd.at[4])
-    out_p.wait()
-
-
-def prior_kernel(st, wp, live, samps_t, img, lp, stv, wpv, hot, scr, imgv, s_in, s_w, s_out):
+    put_prior(c, 4).wait()
+    put_prior(1 - c, 5).wait()
+
+
+def prior_kernel(st, wp, live, samps_t, img, lp, stv, wpv, hot, scr, imgv, la, lb, s_in, s_w, s_out):
     def part(s):
         return pl.ds(pl.multiple_of(s * 128, 128), 128)
 
@@ -475,12 +483,15 @@
         return pltpu.make_async_copy(imgv.at[part(s)], img.at[part(s)], s_out.at[s])
 
     get_s(0).start()
-    for n in range(4):
-        get_w(n).start()
+    get_w(0).start()
+    get_w(1).start()
     get_s(1).start()
+    get_w(2).start()
+    get_w(3).start()
     E = spread(32, 1024)
     E8 = spread(8, 256)
     cls = (lax.broadcasted_iota(jnp.int32, (256, 1024), 1) % 32).astype(F32)
+    lb[...] = jnp.zeros_like(lb)
 
     def hits(t, u):
         rep = dot(samps_t[t].astype(F32).astype(BF), E, ((0,), (0,)))
@@ -489,41 +500,53 @@
 
     lax.fori_loop(0, STEPS, hits, 0)
 
-    def half(s, u):
-        get_s(s).wait()
-
-        def columns(n, u):
-            @pl.when(s == 0)
-            def _():
-                get_w(n).wait()
-
-            low = jnp.concatenate([stv[b, :, part(s)].reshape(512, 512) for b in range(BLOCKS)], axis=1)
-            rhs = jnp.concatenate([wpv[2 * n + i].reshape(2048, 128) for i in range(2)], axis=1)
-            logits = dot(low, rhs)
-            for t in range(STEPS):
-                scr[:, t, :] = stv[n, t, part(s)].astype(F32)
-            imgv[part(s), :, pl.ds(pl.multiple_of(n * 512, 512), 512)] = scr[...].astype(BF)
-
-            def grouped(v):
-                hi = v.astype(BF)
-                lo = (v - hi.astype(F32)).astype(BF)
-                return dot(E8, hi, ((1,), (1,))) + dot(E8, lo, ((1,), (1,)))
-
-            cols = pl.ds(pl.multiple_of(n * 256, 256), 256)
-            total = jnp.log(grouped(jnp.exp(logits)))
-            hit = grouped(logits * hot[:, part(s), cols].reshape(512, 256).astype(F32))
-            value = hit - total
-            for t in range(STEPS):
-                lp[t, pl.ds(pl.multiple_of(n * 8, 8), 8), part(s)] = jnp.where(
-                    live[:, part(s)] > 0.0, value[:, 128 * t : 128 * t + 128], 0.0
-                )
-            return u
-
-        lax.fori_loop(0, 4, columns, 0)
-        put(s).start()
+    def product(s, n):
+        low = jnp.concatenate([stv[b, :, part(s)].reshape(512, 512) for b in range(BLOCKS)], axis=1)
+        rhs = jnp.concatenate([wpv[2 * n + i].reshape(2048, 128) for i in range(2)], axis=1)
+        return dot(low, rhs)
+
+    def scores(logits, s, n):
+        def grouped(v):
+            hi = v.astype(BF)
+            low = (v - hi.astype(F32)).astype(BF)
+            return dot(E8, hi, ((1,), (1,))) + dot(E8, low, ((1,), (1,)))
+
+        cols = pl.ds(pl.multiple_of(n * 256, 256), 256)
+        total = jnp.log(grouped(jnp.exp(logits)))
+        hit = grouped(logits * hot[:, part(s), cols].reshape(512, 256).astype(F32))
+        value = hit - total
+        for t in range(STEPS):
+            lp[t, pl.ds(pl.multiple_of(n * 8, 8), 8), part(s)] = jnp.where(
+                live[:, part(s)] > 0.0, value[:, 128 * t : 128 * t + 128], 0.0
+            )
+
+    def trip(j, u):
+        @pl.when(j < 2)
+        def _():
+            get_s(j).wait()
+
+            def lay(b, u):
+                for t in range(STEPS):
+                    scr[:, t, :] = stv[b, t, part(j)].astype(F32)
+                cols = pl.ds(pl.multiple_of(b * 512, 512), 512)
+                imgv[part(j), :, cols] = scr[...].astype(BF)
+                return u
+
+            lax.fori_loop(0, BLOCKS, lay, 0)
+            put(j).start()
+            get_w(2 * j).wait()
+            get_w(2 * j + 1).wait()
+
+        s, n = j // 2, 2 * (j % 2)
+        last = (2 * j + 7) % 8
+        la[...] = product(s, n)
+        scores(lb[...], last // 4, last % 4)
+        lb[...] = product(s, n + 1)
+        scores(la[...], s, n)
         return u
 
-    lax.fori_loop(0, 2, half, 0)
+    lax.fori_loop(0, 4, trip, 0)
+    scores(lb[...], 1, 3)
     put(0).wait()
     put(1).wait()
 
@@ -563,7 +586,7 @@
             dma((7,)), dma((2,)), dma((2,)),
             dma((4, 3)), dma((4, 8, 2)),
             dma((5,)), dma((8, 2)),
-            dma((5,)), dma((5,)), dma((5,)),
+            dma((5,)), dma((5,)), dma((6,)),
         ],
         compiler_params=pltpu.CompilerParams(
             collective_id=0, has_side_effects=True, vmem_limit_bytes=63 * 1024 * 1024
@@ -584,6 +607,8 @@
             pltpu.VMEM((4, 256, 1024), BF),
             pltpu.VMEM((128, 4, 512), F32),
             pltpu.VMEM((256, 4, 2048), BF),
+            pltpu.VMEM((512, 256), F32),
+            pltpu.VMEM((512, 256), F32),
             dma((2,)), dma((4,)), dma((2,)),
         ],
         compiler_params=pltpu.CompilerParams(vmem_limit_bytes=60 * 1024 * 1024),

time: 106 us -> 102 us (0.962)
  Pallas kernels: 105 us -> 101 us
    pallas_call x1, Pallas kernels: 88.3 us -> 86 us  [on_device(): pl.pallas_call(gru_kernel, name='gru', out_shape=(jax.ShapeDtypeStruct((4...]
    pallas_call x1, Pallas kernels: 16.9 us -> 14.7 us  [on_device(): pl.pallas_call(prior_kernel, name='prior', out_shape=(jax.ShapeDtypeStruc...]
where the time goes in v3:
time: 102 us; the launch traced here: 101 us
  Pallas kernels  101 us (99%)
    pallas_call x1, Pallas kernels, on_device(): pl.pallas_call(gru_kernel, name='gru', out_shape=(jax.ShapeDtypeStruct((4...  86 us
    pallas_call x1, Pallas kernels, on_device(): pl.pallas_call(prior_kernel, name='prior', out_shape=(jax.ShapeDtypeStruc...  14.7 us

profile of v3, /device:TPU:1, one launch (start us, length us, event | category | flops | bytes accessed | tf_op | source)
XLA Modules:
  0.0 101.4 jit_solution(12099427339952440422)
XLA Ops:
  0.6 86.0 %gru.1 = (bf16[4,4,256,512]{3,2,1,0:T(8,128)(2,1)}, bf16[8,4,4,2,4,16,128]{6,5,4,3,2,1,0:T(8,128)(2,1)}, f32[8,256]{1,0:T(8,128)}) custom-call(f32[256,2048]{1,0:T(8,128)} %deter_h.1, s32[32,256]{1,0:T(8,128)} %bitcast.7, s32[2,128]{1,0:T(2,128)} %bitcast.9, s32[1,128]{1,0:T(1,128)} %counts.1, s32[4,256]{1,0:T(4,128)} %bitcast.8, s32[4,32,256]{2,1,0:T(8,128)} %bitcast.5, ...), custom_call_target="tpu_custom_call" | custom-call | tf_op jit(solution)/shard_map/gru/pallas_call | solution.py:559
  86.7 14.7 %prior.1 = (bf16[256,4,2048]{2,1,0:T(4,128)(2,1)}, f32[4,32,256]{2,1,0:T(8,128)}) custom-call(bf16[4,4,256,512]{3,2,1,0:T(8,128)(2,1)} %get-tuple-element.7.st, bf16[8,4,4,2,4,16,128]{6,5,4,3,2,1,0:T(8,128)(2,1)} %get-tuple-element.8.wp, f32[8,256]{1,0:T(8,128)} %get-tuple-element.9.live, s32[4,32,256]{2,1,0:T(8,128)} %bitcast.6), custom_call_target="tpu_custom_call" | custom-call | tf_op jit(solution)/shard_map/prior/pallas_call | solution.py:595

commit v4 on v3

--- a/solution.py
+++ b/solution.py
@@ -323,11 +323,11 @@
     act_terms(0)
     stage(4, 1)
     stage(3, 2)
-    send_rows(2)
     act_terms(1)
     act_terms(2)
+    stage(6, 0)
+    send_rows(2)
     act_terms(3)
-    stage(6, 0)
     stage(5, 1)
     send_rows(3)
     stage(2, 3)
@@ -406,15 +406,18 @@
             low = h.astype(BF)
             rows = pl.ds(pl.multiple_of(t * 256, 256), 256)
 
-            def gates(p):
-                rhs = jnp.concatenate([WD[b, p, q].reshape(512, 128) for q in range(4)], axis=1)
-                return PRE[b, p, rows, :] + dot(low, rhs)
-
-            cand = jnp.tanh(sig(gates(0)) * gates(1))
-            g = sig(gates(2) - 1.0)
-            new = g * cand + (1.0 - g) * h
-            H[...] = new
-            ST[b % 2, t] = (new * live_col).astype(BF)
+            for e in range(2):
+                cols = slice(256 * e, 256 * e + 256)
+
+                def gates(p):
+                    rhs = [WD[b, p, q].reshape(512, 128) for q in range(2 * e, 2 * e + 2)]
+                    return PRE[b, p, rows, cols] + dot(low, jnp.concatenate(rhs, axis=1))
+
+                cand = jnp.tanh(sig(gates(0)) * gates(1))
+                g = sig(gates(2) - 1.0)
+                new = g * cand + (1.0 - g) * h[:, cols]
+                H[:, cols] = new
+                ST[b % 2, t, :, cols] = (new * live_col).astype(BF)
             return u
 
         lax.fori_loop(0, 2, step, 0)

time: 102 us -> 99.2 us (0.973)
  Pallas kernels: 101 us -> 98.4 us
    pallas_call x1, Pallas kernels: 86 us -> 83.7 us  [on_device(): pl.pallas_call(gru_kernel, name='gru', out_shape=(jax.ShapeDtypeStruct((4...]
where the time goes in v4:
time: 99.2 us; the launch traced here: 99 us
  Pallas kernels  98.4 us (99%)
    pallas_call x1, Pallas kernels, on_device(): pl.pallas_call(gru_kernel, name='gru', out_shape=(jax.ShapeDtypeStruct((4...  83.7 us
    pallas_call x1, Pallas kernels, on_device(): pl.pallas_call(prior_kernel, name='prior', out_shape=(jax.ShapeDtypeStruc...  14.7 us

profile of v4, /device:TPU:1, one launch (start us, length us, event | category | flops | bytes accessed | tf_op | source)
XLA Modules:
  0.0 99.0 jit_solution(11533463127396019842)
XLA Ops:
  0.6 83.7 %gru.1 = (bf16[4,4,256,512]{3,2,1,0:T(8,128)(2,1)}, bf16[8,4,4,2,4,16,128]{6,5,4,3,2,1,0:T(8,128)(2,1)}, f32[8,256]{1,0:T(8,128)}) custom-call(f32[256,2048]{1,0:T(8,128)} %deter_h.1, s32[32,256]{1,0:T(8,128)} %bitcast.7, s32[2,128]{1,0:T(2,128)} %bitcast.9, s32[1,128]{1,0:T(1,128)} %counts.1, s32[4,256]{1,0:T(4,128)} %bitcast.8, s32[4,32,256]{2,1,0:T(8,128)} %bitcast.5, ...), custom_call_target="tpu_custom_call" | custom-call | tf_op jit(solution)/shard_map/gru/pallas_call | solution.py:562
  84.3 14.7 %prior.1 = (bf16[256,4,2048]{2,1,0:T(4,128)(2,1)}, f32[4,32,256]{2,1,0:T(8,128)}) custom-call(bf16[4,4,256,512]{3,2,1,0:T(8,128)(2,1)} %get-tuple-element.7.st, bf16[8,4,4,2,4,16,128]{6,5,4,3,2,1,0:T(8,128)(2,1)} %get-tuple-element.8.wp, f32[8,256]{1,0:T(8,128)} %get-tuple-element.9.live, s32[4,32,256]{2,1,0:T(8,128)} %bitcast.6), custom_call_target="tpu_custom_call" | custom-call | tf_op jit(solution)/shard_map/prior/pallas_call | solution.py:598
